TPU v7x, 256 devices: a whole 4x4x8 slice. The times are simulated.
256 devices in a mesh: img: 4 (over x), seq: 8 (over z_lo, y), tp: 8 (over z_hi, core).
Axes of the slice: x: 4, y: 4, z: 8 (z_hi: 4, z_lo: 2; z = z_hi * 2 + z_lo), core: 2. Of those that a mesh axis runs over, the one named last changes fastest.
Arguments:
- vit_qkv: bfloat16 [4, 4096, 3, 1280], P('img', ('seq', 'tp')), may hold values from -6 to 6
- patch_counts: int32 [4], P('img'), may hold values from 1024 to 4096, as said below
- vit_out_weight: bfloat16 [1280, 1280], replicated, may hold values from -0.15625 to 0.15625
- vit_norm_gain: float32 [1280], replicated, may hold values from 0.25 to 1.75
- merger_weight: bfloat16 [5120, 8192], P(('img', 'seq'), 'tp'), may hold values from -8 to 8
- lm_norm_gain: float32 [8192], P('tp'), may hold values from 0.25 to 1.75
- kv_weight: bfloat16 [8192, 2048], P('tp', ('img', 'seq')), may hold values from -0.0625 to 0.0625
- queries: bfloat16 [4, 4096, 64, 128], P('img', 'seq', 'tp'), may hold values from -6 to 6
- span_kv: bfloat16 [4, 4096, 2, 8, 128], P('img', 'seq', None, 'tp'), may hold values from -6 to 6
Outputs:
- lm_attention: bfloat16 [4, 4096, 64, 128], P('img', 'seq', 'tp')
Inputs may be any that keep to these rules, and one draw needn't show every extreme that they name: `patch_counts`: each count is a multiple of 4, at least 1024, and some image has exactly 4096.
All inputs are finite; a program needn't handle non-finite values.
Results may differ from a plain program's by a relative error of at most 0.04.
Values may be sent and summed in bfloat16 or wider, within the bound.
A program may use at most 128 MiB of HBM per device.

v0:
```python
import jax
import jax.numpy as jnp
from jax import lax
from jax.sharding import Mesh
from jax.sharding import PartitionSpec as P

VIT_D = 1280
VIT_HEADS = 16
VIT_HDIM = 80
D = 8192
HQ = 64
KVH = 8
HD = 128
SEQ = ("seq_0", "seq_1")
IMG_SEQ = ("img", "seq_0", "seq_1")
SEQ_TP = ("seq_0", "seq_1", "tp")


masked_score = -1e30


def sent_to_all(x, axis):
    copies = jnp.broadcast_to(x, (lax.axis_size(axis), *x.shape))
    return lax.all_to_all(copies, axis, split_axis=0, concat_axis=0, tiled=True)


def in_order(parts, dim):
    parts = jnp.moveaxis(parts, 0, dim)
    lengths = parts.shape
    return parts.reshape(*lengths[:dim], lengths[dim] * lengths[dim + 1], *lengths[dim + 2 :])


def gather_directly(x, axis, dim):
    parts = sent_to_all(x, axis)
    return in_order(parts, dim)


def in_one_piece(arrays, axis, dim, along):
    ends, at = ([], 0)
    for a in arrays[:-1]:
        at += a.shape[along]
        ends.append(at)
    both = jnp.concatenate(arrays, axis=along)
    return tuple(jnp.split(gather_directly(both, axis, dim), ends, axis=along))


def all_blocks(x, axes, sequence):
    parts = x[None]
    for k in sequence:
        parts = lax.all_gather(parts, axes[k], axis=0, tiled=True)
    current = [lax.axis_size(axes[k]) for k in reversed(sequence)]
    parts = parts.reshape(*current, *x.shape)
    turned = sorted(range(len(sequence)), key=lambda place: sequence[len(sequence) - 1 - place])
    return parts.transpose(*turned, *range(len(sequence), parts.ndim)).reshape(-1, *x.shape)


def gathered_by_axis(x, axes, sequence, dim):
    return in_order(all_blocks(x, axes, sequence), dim)


def over_copies(x, axis):
    return sent_to_all(x, axis).sum(axis=0)


def in_blocks(x, dim, length):
    before, after = (x.shape[:dim], x.shape[dim + 1 :])
    return jnp.moveaxis(x.reshape(*before, length, -1, *after), dim, 0)


def sum_at_owner(x, axis, dim):
    length = lax.axis_size(axis)
    parts = lax.all_to_all(in_blocks(x, dim, length), axis, 0, 0, tiled=True)
    return jnp.sum(parts.astype(jnp.float32), axis=0)


def in_one_piece_2(arrays, axis, dim, along):
    widths = [a.shape[along] for a in arrays]
    both = jnp.concatenate(arrays, axis=along)
    out = lax.all_gather(both, axis, axis=dim, tiled=True)
    return tuple(jnp.split(out, [sum(widths[:k]) for k in range(1, len(widths))], axis=along))


def fold_block(running, scores, usable, value_block, forms):
    peak, weight_sum, blended = running
    scores = jnp.where(usable, scores, masked_score)
    new_peak = jnp.maximum(peak, jnp.max(scores, axis=-1))
    weights = jnp.where(usable, jnp.exp(scores - new_peak[..., None]), 0.0)
    decay = jnp.exp(peak - new_peak)
    weight_sum = weight_sum * decay + jnp.sum(weights, axis=-1)
    blended = blended * decay[..., None] + jnp.einsum(
        forms, weights.astype(jnp.bfloat16), value_block, preferred_element_type=jnp.float32
    )
    return (new_peak, weight_sum, blended)


def local(
    vit_qkv,
    patch_counts,
    vit_out_weight,
    vit_norm_gain,
    merger_weight,
    lm_norm_gain,
    kv_weight,
    queries,
    span_kv,
):
    patch_rows = vit_qkv.shape[1]
    tp_count = lax.axis_size("tp")
    seq_index = lax.axis_index(SEQ)
    tp_index = lax.axis_index("tp")
    patch_total = patch_counts[0]
    local_qkv = vit_qkv[0].reshape(patch_rows, 3, VIT_HEADS, VIT_HDIM)
    scaling = VIT_HDIM ** (-0.5)
    spread = lax.all_to_all(local_qkv, SEQ, split_axis=2, concat_axis=0, tiled=True)
    local_rows = spread.shape[0]

    def seq_rows(index):
        source = index // local_rows
        within = index % local_rows
        return (within // patch_rows * tp_count + source) * patch_rows + within % patch_rows

    heads_local = spread.shape[2]
    query_count = spread.shape[0]
    query_rows = spread[:, 0]
    running = (
        jnp.full((heads_local, query_count), masked_score, jnp.float32),
        jnp.zeros((heads_local, query_count), jnp.float32),
        jnp.zeros((heads_local, query_count, VIT_HDIM), jnp.float32),
    )
    make_heads_local = query_rows.shape[1]
    key_piece, value_piece = in_one_piece((spread[:, 1], spread[:, 2]), "tp", 0, 1)
    blocks = key_piece.shape[0] // local_rows
    key_blocks = key_piece.reshape(blocks, local_rows, make_heads_local, VIT_HDIM)
    value_blocks = value_piece.reshape(blocks, local_rows, make_heads_local, VIT_HDIM)
    offsets = jnp.arange(blocks, dtype=jnp.int32) * local_rows

    def make_advance(state, inputs):
        key_block, value_block, offset = inputs
        usable = seq_rows(offset + jnp.arange(local_rows, dtype=jnp.int32)) < patch_total
        scores = (
            jnp.einsum("qhd,khd->hqk", query_rows, key_block, preferred_element_type=jnp.float32)
            * scaling
        )
        return (fold_block(state, scores, usable[None, None, :], value_block, "hqk,khd->hqd"), None)

    result, _ = lax.scan(make_advance, running, (key_blocks, value_blocks, offsets))
    state = result
    peak, weight_sum, blended = state
    returned = lax.all_to_all(
        jnp.transpose(blended / weight_sum[..., None], (1, 0, 2)).astype(jnp.bfloat16),
        SEQ,
        split_axis=0,
        concat_axis=1,
        tiled=True,
    )
    attended = returned.reshape(patch_rows, VIT_D)
    hidden = jnp.dot(attended, vit_out_weight, preferred_element_type=jnp.float32)
    patch_ids = (seq_index * tp_count + tp_index) * patch_rows + jnp.arange(
        patch_rows, dtype=jnp.int32
    )
    hidden = jnp.where((patch_ids < patch_total)[:, None], hidden, 0.0)
    centred = hidden - jnp.mean(hidden, axis=-1, keepdims=True)
    spread_sq = jnp.mean(centred * centred, axis=-1, keepdims=True)
    normed = (centred * lax.rsqrt(spread_sq + 1e-06) * vit_norm_gain).astype(jnp.bfloat16)
    merged_local = normed.reshape(patch_rows // 4, 4 * VIT_D)
    token_rows = gather_directly(merged_local, "tp", 0)
    embedded_sum = jnp.dot(
        token_rows,
        gathered_by_axis(merger_weight, IMG_SEQ, (1, 0, 2), 0),
        preferred_element_type=jnp.float32,
    )
    embedded = lax.optimization_barrier(embedded_sum.astype(jnp.bfloat16))
    embedded_wide = embedded.astype(jnp.float32)
    square_sums = over_copies(jnp.sum(embedded_wide * embedded_wide, axis=-1), "tp")
    lm_normed = (embedded_wide * lax.rsqrt(square_sums[:, None] / D + 1e-06) * lm_norm_gain).astype(
        jnp.bfloat16
    )
    kv_terms = jnp.dot(
        lm_normed,
        lax.all_gather(kv_weight, IMG_SEQ, axis=1, tiled=True),
        preferred_element_type=jnp.float32,
    )
    visual_count = kv_terms.shape[0]
    kv_terms = kv_terms.reshape(visual_count, 2, KVH, HD)
    visual_kv = sum_at_owner(kv_terms.astype(jnp.bfloat16), "tp", 2).astype(jnp.bfloat16)
    span_rows = queries.shape[1]
    kv_local = span_kv.shape[3]
    groups = HQ // KVH
    lm_scaling = HD ** (-0.5)
    grouped = queries[0].reshape(span_rows, kv_local, groups, HD)
    causal = jnp.arange(span_rows)[:, None] >= jnp.arange(span_rows)[None, :]
    near_scores = (
        jnp.einsum("ckgd,nkd->kgcn", grouped, span_kv[0, :, 0], preferred_element_type=jnp.float32)
        * lm_scaling
    )
    initial = (
        jnp.full((kv_local, groups, span_rows), masked_score, jnp.float32),
        jnp.zeros((kv_local, groups, span_rows), jnp.float32),
        jnp.zeros((kv_local, groups, span_rows, HD), jnp.float32),
    )
    initial = fold_block(
        initial, near_scores, causal[None, None], span_kv[0, :, 1], "kgcn,nkd->kgcd"
    )
    visual_total = patch_total // 4
    key_piece, value_piece = in_one_piece_2((visual_kv[:, 0], visual_kv[:, 1]), SEQ, 0, 1)
    blocks = key_piece.shape[0] // visual_count
    key_blocks = key_piece.reshape(blocks, visual_count, kv_local, HD)
    value_blocks = value_piece.reshape(blocks, visual_count, kv_local, HD)
    offsets = jnp.arange(blocks, dtype=jnp.int32) * visual_count

    def visual_advance(state, inputs):
        key_block, value_block, offset = inputs
        usable = offset + jnp.arange(visual_count, dtype=jnp.int32) < visual_total
        scores = (
            jnp.einsum("ckgd,nkd->kgcn", grouped, key_block, preferred_element_type=jnp.float32)
            * lm_scaling
        )
        return (
            fold_block(state, scores, usable[None, None, None, :], value_block, "kgcn,nkd->kgcd"),
            None,
        )

    result, _ = lax.scan(visual_advance, initial, (key_blocks, value_blocks, offsets))
    peak, weight_sum, blended = result
    result = jnp.transpose(blended / weight_sum[..., None], (2, 0, 1, 3))
    return result.reshape(span_rows, kv_local * groups, HD).astype(jnp.bfloat16)[None]


def solution(mesh):
    torus = Mesh(
        mesh.devices.reshape(mesh.shape["img"], 2, 4, mesh.shape["tp"]),
        ("img", "seq_0", "seq_1", "tp"),
    )
    placed = (
        P("img", SEQ_TP, None, None),
        P("img"),
        P(),
        P(),
        P(IMG_SEQ, "tp"),
        P("tp"),
        P("tp", IMG_SEQ),
        P("img", SEQ, "tp", None),
        P("img", SEQ, None, "tp", None),
    )
    return jax.shard_map(
        local, mesh=torus, in_specs=placed, out_specs=P("img", SEQ, "tp", None), check_vma=False
    )
```

profile of v0, /device:TPU:8, one launch (start us, length us, event | category | flops | bytes accessed | tf_op | source)
XLA Modules:
  0.0 450.2 jit_solution(11617065756509815237)
XLA Ops:
  6.5 12.6 %all-gather = bf16[320,1024]{1,0:T(8,128)(2,1)} all-gather(bf16[160,1024]{1,0:T(8,128)(2,1)} %param.17), channel_id=2, replica_groups=mesh['img'=4,'seq_0'=2,'seq_1'=4,'tp'=8] {'seq_0'}, dimensions={0}, use_global_device_ids=true | all-gather | bytes 983040 | tf_op jit(solution)/shard_map/all_gather | solution.py:50
  19.2 39.7 %all-gather.5.cloned.1.call-done = bf16[8,160,1024]{2,1,0:T(8,128)(2,1)} async-done(((bf16[2,160,1024]{2,1,0:T(8,128)(2,1)}), bf16[8,160,1024]{2,1,0:T(8,128)(2,1)}) %all-gather.5.cloned.1.call-update) | async-done | bytes 2621456 | tf_op jit(solution)/shard_map/all_gather | solution.py:50
  59.0 2.8 reshape_squeeze.6
  63.1 16.7 %all_to_all.54 = bf16[64,3,16,80]{3,0,1,2:T(8,128)(2,1)} all-to-all(bf16[64,3,16,80]{3,0,1,2:T(8,128)(2,1)S(1)} %copy.154), channel_id=1, replica_groups=mesh['img'=4,'seq_0'=2,'seq_1'=4,'tp'=8] {'seq_0','seq_1'}, dimensions={2} | all-to-all | bytes 983040 | tf_op jit(solution)/shard_map/all_to_all | solution.py:114
  87.6 6.1 %all-to-all-start.1 = ((bf16[8,512,4,80]{1,3,2,0:T(8,128)(2,1)}), bf16[8,512,4,80]{1,3,2,0:T(8,128)(2,1)}, u32[]{:S(2)}, u32[]{:S(2)}) async-start(bf16[8,512,4,80]{1,3,2,0:T(8,128)(2,1)} %broadcast_in_dim.148), calls=%async_computation.1 | async-start | bytes 5242880 | tf_op jit(solution)/shard_map/all_to_all | solution.py:24
  94.4 62.4 %all-to-all-done.1 = bf16[8,512,4,80]{1,3,2,0:T(8,128)(2,1)} async-done(((bf16[8,512,4,80]{1,3,2,0:T(8,128)(2,1)}), bf16[8,512,4,80]{1,3,2,0:T(8,128)(2,1)}, u32[]{:S(2)}, u32[]{:S(2)}) %all-to-all-start.1) | async-done | bytes 2621472 | tf_op jit(solution)/shard_map/all_to_all | solution.py:24
  160.9 76.3 %while.33 = (s32[]{:T(128)}, f32[2,512]{1,0:T(2,128)S(1)}, f32[2,512]{1,0:T(2,128)S(1)}, f32[2,512,80]{1,2,0:T(8,128)}, s32[8]{0:T(128)S(1)}, /*index=5*/s32[]{:...) while((s32[]{:T(128)}, f32[2,512]{1,0:T(2,128)S(1)}, ...), condition=%wide.region_5.6_spmd.clone, body=%wide.region_2.5_spmd.clone.sunk | while | flops 174861312 | bytes 15896233 | solution.py:146
  162.8 2.8 bitcast_reduce_fusion.5
  181.7 2.8 bitcast_reduce_fusion.5
  191.3 2.8 bitcast_reduce_fusion.5
  200.8 2.8 bitcast_reduce_fusion.5
  210.4 2.8 bitcast_reduce_fusion.5
  219.9 2.8 bitcast_reduce_fusion.5
  229.5 2.8 bitcast_reduce_fusion.5
  239.0 4.4 all-to-all-start.2
  244.1 5.6 %all-to-all-done.2 = bf16[512,2,80]{2,1,0:T(2,128)(2,1)S(1)} async-done(((bf16[512,2,80]{2,1,0:T(2,128)(2,1)}), bf16[512,2,80]{2,1,0:T(2,128)(2,1)S(1)}, u32[]{:S(2)}, u32[]{:S(2)}) %all-to-all-start.2) | async-done | bytes 163872 | tf_op jit(solution)/shard_map/all_to_all | solution.py:149
  256.3 3.9 all-to-all-start.3
  261.4 4.9 %fusion.55 = (f32[8,512]{1,0:T(8,128)S(1)}, f32[512,512,8]{1,0,2:T(8,128)}) fusion(pred[512,512]{0,1:T(8,128)(4,1)S(1)} %iota_compare_fusion, bf16[512,8,128]{2,1,0:T(8,128)(2,1)S(1)} %bitcast.250, bf16[1,512,1,1,128]{4,2,3,1,0:T(2,128)(2,1)S(1)} %get-tuple-element.403), kind=kOutput, calls=%fused_computation.84 | convolution fusion | flops 543158272 | bytes 9846784 | tf_op jit(solution)/shard_map/ckgd,nkd->kgcn/dot_general | solution.py:193
  266.3 9.8 %copy.165 = bf16[4,2,4,160,1024]{4,3,2,1,0:T(8,128)(2,1)} copy(bf16[4,2,4,160,1024]{4,3,1,0,2:T(8,128)(2,1)} %bitcast.243) | data formatting | bytes 20971520 | tf_op jit(solution)/shard_map/transpose | solution.py:54
  276.2 19.0 %all-to-all-done.3 = bf16[8,16,5120]{2,1,0:T(8,128)(2,1)S(1)} async-done(((bf16[8,16,5120]{2,1,0:T(8,128)(2,1)}), bf16[8,16,5120]{2,1,0:T(8,128)(2,1)S(1)}, u32[]{:S(2)}, u32[]{:S(2)}) %all-to-all-start.3) | async-done | bytes 1310752 | tf_op jit(solution)/shard_map/all_to_all | solution.py:24
  295.1 5.5 %convolution_convert_fusion.1 = bf16[128,1024]{1,0:T(8,128)(2,1)S(1)} fusion(bf16[128,5120]{1,0:T(8,128)(2,1)S(1)} %bitcast.247, bf16[5120,1024]{1,0:T(8,128)(2,1)} %bitcast.241), kind=kOutput, calls=%fused_computation.98 | convolution fusion | flops 1342308352 | bytes 12058624 | tf_op jit(solution)/shard_map/dot_general | solution.py:167
  301.4 3.3 all-to-all-start.4
  304.7 4.5 %fusion.57 = f32[8,512]{1,0:T(8,128)S(1)} fusion(f32[512,512,8]{1,0,2:T(8,128)} %get-tuple-element.412, f32[8,512]{1,0:T(8,128)S(1)} %get-tuple-element.408, pred[512,512]{0,1:T(8,128)(4,1)S(1)} %iota_compare_fusion), kind=kLoop, calls=%fused_computation.86 | loop fusion | flops 10481664 | bytes 8683520 | tf_op jit(solution)/shard_map/reduce_sum | solution.py:89
  309.3 3.0 all-to-all-done.4
  312.3 24.4 %all-gather.9.cloned.1.call-done = bf16[1024,2048]{0,1:T(8,128)(2,1)} async-done(((bf16[1024,64]{0,1:T(8,128)(2,1)}), bf16[1024,2048]{0,1:T(8,128)(2,1)}) %all-gather.9.cloned.1.call-update) | async-done | bytes 4194320 | tf_op jit(solution)/shard_map/all_gather | solution.py:180
  336.7 3.7 fusion.65
  341.8 4.8 %all-to-all-start.5 = ((bf16[8,128,2,1,128]{4,2,1,3,0:T(2,128)(2,1)}), bf16[8,128,2,1,128]{4,2,1,3,0:T(2,128)(2,1)}, u32[]{:S(2)}, u32[]{:S(2)}) async-start(bf16[8,128,2,1,128]{4,2,1,3,0:T(2,128)(2,1)} %bitcast.189), calls=%async_computation.5 | async-start | bytes 1048576 | tf_op jit(solution)/shard_map/all_to_all | solution.py:72
  346.8 7.4 %add_bitcast_fusion = f32[1,8,512,128]{3,2,1,0:T(8,128)} fusion(f32[512,512,8]{1,0,2:T(8,128)} %get-tuple-element.412, f32[8,512]{1,0:T(8,128)S(1)} %get-tuple-element.408, pred[512,512]{0,1:T(8,128)(4,1)S(1)} %iota_compare_fusion, f32[8,512]{1,0:T(8,128)S(1)} %get-tuple-element.406, bf16[1,512,1,1,128]{4,2,3,1,0:T(2,128)(2,1)S(1)} %copy-done.7), kind=kOutput, calls=%fused_computation.94 | convolution fusion | flops 547880960 | bytes 10911744 | tf_op jit(solution)/shard_map/kgcn,nkd->kgcd/dot_general | solution.py:90
  354.2 6.4 %all-to-all-done.5 = bf16[8,128,2,1,128]{4,2,1,3,0:T(2,128)(2,1)} async-done(((bf16[8,128,2,1,128]{4,2,1,3,0:T(2,128)(2,1)}), bf16[8,128,2,1,128]{4,2,1,3,0:T(2,128)(2,1)}, u32[]{:S(2)}, u32[]{:S(2)}) %all-to-all-start.5) | async-done | bytes 524320 | tf_op jit(solution)/shard_map/all_to_all | solution.py:72
  362.2 27.0 %all_gather.19 = bf16[1024,2,128]{2,0,1:T(8,128)(2,1)S(1)} all-gather(bf16[128,2,128]{2,0,1:T(8,128)(2,1)S(1)} %pad_maximum_fusion.1), channel_id=1, replica_groups=mesh['img'=4,'seq_0'=2,'seq_1'=4,'tp'=8] {'seq_0','seq_1'}, dimensions={0}, use_global_device_ids=true | all-gather | bytes 589824 | tf_op jit(solution)/shard_map/all_gather | solution.py:79
  390.0 49.6 %while.32 = (s32[]{:T(128)}, f32[1,8,512]{2,1,0:T(8,128)S(1)}, f32[1,8,512]{2,1,0:T(8,128)S(1)}, f32[1,8,512,128]{3,2,1,0:T(8,128)}, s32[8]{0:T(128)S(1)}, /*ind...) while((s32[]{:T(128)}, f32[1,8,512]{2,1,0:T(8,128)S(1)}, ...), condition=%wide.region_14.15_spmd, body=%wide.region_11.14_spmd.sunk | while | flops 276312320 | bytes 28641840 | solution.py:223
  439.7 3.9 fusion.68
  (235 shorter events, 134.2 us)
Async XLA Ops:
  6.5 246.3 %copy-start = (bf16[1280,1280]{1,0:T(8,128)(2,1)S(1)}, bf16[1280,1280]{1,0:T(8,128)(2,1)}, u32[]{:S(2)}) copy-start(bf16[1280,1280]{1,0:T(8,128)(2,1)} %param.15) | copy-start | bytes 9830404
  6.5 52.4 %all-gather.5.cloned.1.call-start = ((), (), s32[]{:S(2)}) async-start(), calls=%async_computation.6 | async-start | bytes 3276800 | tf_op jit(solution)/shard_map/all_gather | solution.py:50
  19.1 247.2 %all-gather.7.cloned.1.call-start = ((), (), s32[]{:S(2)}) async-start(), calls=%async_computation.7 | async-start | bytes 13107200 | tf_op jit(solution)/shard_map/all_gather | solution.py:50
  87.6 69.3 %all-to-all-start.1 = ((bf16[8,512,4,80]{1,3,2,0:T(8,128)(2,1)}), bf16[8,512,4,80]{1,3,2,0:T(8,128)(2,1)}, u32[]{:S(2)}, u32[]{:S(2)}) async-start(bf16[8,512,4,80]{1,3,2,0:T(8,128)(2,1)} %broadcast_in_dim.148), calls=%async_computation.1 | async-start | bytes 5242880 | tf_op jit(solution)/shard_map/all_to_all | solution.py:24
  93.7 243.1 %all-gather.9.cloned.1.call-start = ((), (), s32[]{:S(2)}) async-start(), calls=%async_computation.8 | async-start | bytes 4325376 | tf_op jit(solution)/shard_map/all_gather | solution.py:180
  165.5 2.4 copy-start.2
  174.9 2.4 copy-start.2
  184.5 2.4 copy-start.2
  194.0 2.4 copy-start.2
  203.6 2.4 copy-start.2
  213.1 2.4 copy-start.2
  222.7 2.4 copy-start.2
  232.3 2.4 copy-start.2
  239.0 10.6 %all-to-all-start.2 = ((bf16[512,2,80]{2,1,0:T(2,128)(2,1)}), bf16[512,2,80]{2,1,0:T(2,128)(2,1)S(1)}, u32[]{:S(2)}, u32[]{:S(2)}) async-start(bf16[512,2,80]{2,1,0:T(2,128)(2,1)} %bitcast.256), calls=%async_computation.2 | async-start | bytes 524288 | tf_op jit(solution)/shard_map/all_to_all | solution.py:149
  252.9 2.0 copy-start.8
  255.1 5.2 %copy-start.6 = (bf16[1,512,2,1,128]{4,2,3,1,0:T(2,128)(2,1)S(1)}, bf16[1,512,2,1,128]{4,2,3,1,0:T(2,128)(2,1)}, u32[]{:S(2)}) copy-start(bf16[1,512,2,1,128]{4,2,3,1,0:T(2,128)(2,1)} %param.21) | copy-start | bytes 786436
  256.3 5.1 %copy-start.5 = (bf16[1,512,8,128]{3,2,1,0:T(8,128)(2,1)S(1)}, bf16[1,512,8,128]{3,2,1,0:T(8,128)(2,1)}, u32[]{:S(2)}) copy-start(bf16[1,512,8,128]{3,2,1,0:T(8,128)(2,1)} %param.20) | copy-start | bytes 3145732
  256.3 38.8 %all-to-all-start.3 = ((bf16[8,16,5120]{2,1,0:T(8,128)(2,1)}), bf16[8,16,5120]{2,1,0:T(8,128)(2,1)S(1)}, u32[]{:S(2)}, u32[]{:S(2)}) async-start(bf16[8,16,5120]{2,1,0:T(8,128)(2,1)} %broadcast_in_dim.150), calls=%async_computation.3 | async-start | bytes 2621440 | tf_op jit(solution)/shard_map/all_to_all | solution.py:24
  301.4 10.9 %all-to-all-start.4 = ((f32[8,1,128]{2,1,0:T(1,128)}), f32[8,1,128]{2,1,0:T(1,128)S(1)}, u32[]{:S(2)}, u32[]{:S(2)}) async-start(f32[8,1,128]{2,1,0:T(1,128)} %broadcast_in_dim.152), calls=%async_computation.4 | async-start | bytes 8192 | tf_op jit(solution)/shard_map/all_to_all | solution.py:24
  304.7 32.0 %copy-start.9 = (f32[1024]{0:T(1024)S(1)}, f32[1024]{0:T(1024)}, u32[]{:S(2)}) copy-start(f32[1024]{0:T(1024)} %param.18) | copy-start | bytes 12292
  340.6 6.2 %copy-start.7 = (bf16[1,512,1,1,128]{4,2,3,1,0:T(2,128)(2,1)S(1)}, bf16[1,512,1,1,128]{4,2,3,1,0:T(2,128)(2,1)}, u32[]{:S(2)}) copy-start(bf16[1,512,1,1,128]{4,2,3,1,0:T(2,128)(2,1)} %get-tuple-element.402) | copy-start | bytes 393220
  341.8 18.8 %all-to-all-start.5 = ((bf16[8,128,2,1,128]{4,2,1,3,0:T(2,128)(2,1)}), bf16[8,128,2,1,128]{4,2,1,3,0:T(2,128)(2,1)}, u32[]{:S(2)}, u32[]{:S(2)}) async-start(bf16[8,128,2,1,128]{4,2,1,3,0:T(2,128)(2,1)} %bitcast.189), calls=%async_computation.5 | async-start | bytes 1048576 | tf_op jit(solution)/shard_map/all_to_all | solution.py:72
  390.0 2.5 copy-start.3
  394.9 1.3 copy-start.4
  396.2 2.6 copy-start.3
  402.4 2.6 copy-start.3
  408.6 2.6 copy-start.3
  414.8 2.6 copy-start.3
  421.0 2.6 copy-start.3
  427.2 2.6 copy-start.3
  433.4 2.6 copy-start.3
  439.6 4.0 copy-start.1
  (7 other events, 9.3 us)
Sparse Core Ops, SparseCore 0:
  19.3 39.6 all-gather.4
  60.7 103.4 all-gather.6
  166.1 170.6 all-gather.8
where the time goes:
time: 457 us; the launch traced here: 450 us
  waiting for transfers between devices  161 us (35%)
  matrix products  92.9 us (20%)
  blocking collectives  56.2 us (12%)
  local copies, waits for them, and re-layouts  51.2 us (11%)
  other arithmetic  51.2 us (11%)
  starting transfers between devices  22.6 us (5%)
  between operations  14.1 us (3%)
    all_to_all x3, waiting for transfers between devices, sent_to_all(): return lax.all_to_all(copies, axis, split_axis=0, concat_axis=0, tiled=True)  84.3 us
    dot_general x17, matrix products, fold_block(): jnp.einsum(forms, weights.astype(jnp.bfloat16), value_block, preferred_el...  45.3 us
    all_gather x2, waiting for transfers between devices, all_blocks(): parts = lax.all_gather(parts, axes[k], axis=0, tiled=True)  39.8 us
    reduce_sum x17, other arithmetic, fold_block(): weight_sum = weight_sum * decay + jnp.sum(weights, axis=-1)  28.1 us
    all_gather x1, blocking collectives, in_one_piece_2(): out = lax.all_gather(both, axis, axis=dim, tiled=True)  27 us
    all_gather x1, waiting for transfers between devices, local(): lax.all_gather(kv_weight, IMG_SEQ, axis=1, tiled=True)  24.4 us
    dot_general x8, matrix products, make_advance(): jnp.einsum('qhd,khd->hqk', query_rows, key_block, preferred_element_type=...  22 us
    all_to_all x1, blocking collectives, local(): lax.all_to_all(local_qkv, SEQ, split_axis=2, concat_axis=0, tiled=True)  16.7 us
  transfers between devices with their start and end apart: 8, of which 7 were waited for; matrix products, arithmetic and copies ran while one was open for 29% of the time, Pallas kernels for 0%

commit v1 on v0

v1 whole, which is shorter than its diff:
```python
import jax
import jax.numpy as jnp
from jax import lax
from jax.experimental import pallas as pl
from jax.experimental.pallas import tpu as pltpu
from jax.sharding import Mesh
from jax.sharding import PartitionSpec as P

VIT_D = 1280
VIT_HEADS = 16
VIT_HDIM = 80
D = 8192
HQ = 64
KVH = 8
HD = 128
SEQ = ("zl", "y")
TP = ("zh", "c")
IMG_SEQ = ("x", "zl", "y")
MASKED = -1e30
LOG2E = 1.4426950408889634
F32 = jnp.float32
BF16 = jnp.bfloat16

ONE_AT, MASK_AT, KEY_AT, QUERY_AT, PACKED = 80, 81, 82, 162, 256
RING_ORDER = (0, 1, 7, 2, 6, 3, 5, 4)


def remote(src, dst, send_sem, recv_sem, **device):
    return pltpu.make_async_remote_copy(
        src_ref=src,
        dst_ref=dst,
        send_sem=send_sem,
        recv_sem=recv_sem,
        device_id=device,
        device_id_type=pl.DeviceIdType.MESH,
    )


def mod(a, n):
    return lax.rem(a, n)


def meet(peers):
    barrier = pltpu.get_barrier_semaphore()
    for device in peers:
        pl.semaphore_signal(
            barrier, inc=1, device_id=device, device_id_type=pl.DeviceIdType.MESH
        )
    pl.semaphore_wait(barrier, len(peers))


def nt_dot(a, b):
    return lax.dot_general(a, b, (((1,), (1,)), ((), ())), preferred_element_type=F32)


def vit_kernel(
    packed, wo, gain, live, tok_out,
    kv, qp, acc, peak, back, att, wov, nf, slab, mid, tok,
    a_s, a_r, y1_s, y1_r, y2_s, y2_r, o_s, o_r, m_s, m_r, t_s, t_r, w_sem, out_sem,
):
    y, zh, zl, c = (lax.axis_index(a) for a in ("y", "zh", "zl", "c"))
    z = zh * 2 + zl
    me = z * 2 + c
    up, down, across = mod(y + 1, 4), mod(y + 3, 4), mod(y + 2, 4)

    def place(dz, dc):
        other = mod(z + dz, 8)
        return other, mod(c + dc, 2)

    def device_of(other_z, other_c):
        return {"zh": lax.div(other_z, 2), "zl": mod(other_z, 2), "c": other_c}

    order = [(dz, dc) for dz in RING_ORDER for dc in range(2)]
    peers = [device_of(*place(dz, dc)) for dz, dc in order if (dz, dc) != (0, 0)]
    peers += [{"y": up}, {"y": down}, {"y": across}]
    meet(peers)

    sends = []
    for dz in (4, 3, 5, 2, 6, 1, 7, 0):
        for dc in range(2):
            if (dz, dc) == (0, 0):
                continue
            oz, oc = place(dz, dc)
            k = dz * 2 + dc
            copy = remote(
                packed.at[oz * 2 + oc], kv.at[y, me], a_s.at[k], a_r.at[k], **device_of(oz, oc)
            )
            copy.start()
            sends.append(copy)
    weights = []
    for h in range(VIT_HEADS):
        copy = pltpu.make_async_copy(
            wo.at[pl.ds(h * VIT_HDIM, VIT_HDIM)], wov.at[h, pl.ds(0, VIT_HDIM)], w_sem.at[h]
        )
        copy.start()
        weights.append(copy)
    kv[y, me] = packed[me]
    for h in range(VIT_HEADS):
        wov[h, VIT_HDIM:, :] = jnp.zeros((HD - VIT_HDIM, VIT_D), BF16)

    for i, (dz, dc) in enumerate(order):
        k = dz * 2 + dc
        source = mod(z + 8 - dz, 8) * 2 + mod(c + dc, 2)
        if k == 0:
            block = packed.at[me]
        else:
            block = kv.at[y, source]
            remote(block, block, a_s.at[k], a_r.at[k], y=up).wait_recv()
        for way, target in ((0, up), (1, down)):
            copy = remote(block, kv.at[y, source], y1_s.at[way, i], y1_r.at[way, i], y=target)
            copy.start()
            sends.append(copy)

    row = lax.broadcasted_iota(jnp.int32, (PACKED, PACKED), 0)
    col = lax.broadcasted_iota(jnp.int32, (PACKED, PACKED), 1)
    moved = (col >= KEY_AT) & (col < QUERY_AT) & (row == col + (QUERY_AT - KEY_AT))
    pick = moved | ((col == MASK_AT) & (row == ONE_AT))
    pick = jnp.where(pick, 1.0, 0.0).astype(BF16)
    scale = VIT_HDIM**-0.5 * LOG2E

    def fold(tile, slot, first):
        rows = pl.ds(pl.multiple_of(tile * 256, 256), 256)
        block = kv[slot].reshape(1024, PACKED)
        scores = nt_dot(qp[rows, :], block)
        top = jnp.max(scores, axis=1, keepdims=True)
        if first:
            weights = jnp.exp2((scores - top) * scale)
            total = jnp.dot(weights.astype(BF16), block, preferred_element_type=F32)
        else:
            old = peak[rows, :][:, :1]
            top = jnp.maximum(old, top)
            weights = jnp.exp2((scores - top) * scale)
            total = jnp.dot(weights.astype(BF16), block, preferred_element_type=F32)
            total += acc[rows, :] * jnp.exp2((old - top) * scale)
        peak[rows, :] = jnp.broadcast_to(top, (256, HD))
        return rows, total

    def whole(slot, first):
        def step(tile, carry):
            rows, total = fold(tile, slot, first)
            acc[rows, :] = total
            return carry

        lax.fori_loop(0, 4, step, 0)

    qp[...] = jnp.dot(
        kv[y].reshape(1024, PACKED), pick, preferred_element_type=F32
    ).astype(BF16)
    whole(y, True)

    for i, (dz, dc) in enumerate(order):
        source = mod(z + 8 - dz, 8) * 2 + mod(c + dc, 2)
        way, origin, target = ((0, down, up), (1, up, down))[i % 2]
        block = kv.at[origin, source]
        remote(block, block, y1_s.at[way, i], y1_r.at[way, i], y=up).wait_recv()
        copy = remote(block, block, y2_s.at[i], y2_r.at[i], y=target)
        copy.start()
        sends.append(copy)
    for i, (dz, dc) in enumerate(order):
        source = mod(z + 8 - dz, 8) * 2 + mod(c + dc, 2)
        way, origin = ((1, up), (0, down))[i % 2]
        block = kv.at[origin, source]
        remote(block, block, y1_s.at[way, i], y1_r.at[way, i], y=up).wait_recv()
    whole(down, False)
    whole(up, False)
    for i, (dz, dc) in enumerate(order):
        source = mod(z + 8 - dz, 8) * 2 + mod(c + dc, 2)
        block = kv.at[across, source]
        remote(block, block, y2_s.at[i], y2_r.at[i], y=up).wait_recv()

    def last(t, carry):
        tile = mod(zh + 1 + t, 4)
        _, total = fold(tile, across, False)
        done = (total[:, :HD] / total[:, ONE_AT : ONE_AT + 1]).astype(BF16)
        back[pl.ds(tile * 4, 4)] = done.reshape(4, 64, HD)
        for dzl in range(2):
            for dc in range(2):
                ozl, oc = mod(zl + dzl, 2), mod(c + dc, 2)
                k = t * 4 + dzl * 2 + dc
                copy = remote(
                    back.at[tile * 4 + ozl * 2 + oc], att.at[me], o_s.at[k], o_r.at[k],
                    zh=tile, zl=ozl, c=oc,
                )
                if dzl == 0 and dc == 0:
                    pl.when(t < 3)(copy.start)
                else:
                    copy.start()
        return carry

    lax.fori_loop(0, 4, last, 0)
    att[me] = back[me]
    for copy in weights:
        copy.wait()
    for t in range(4):
        for dzl in range(2):
            for dc in range(2):
                if (t, dzl, dc) == (3, 0, 0):
                    continue
                source = mod(zh + 3 - t, 4) * 4 + mod(zl + dzl, 2) * 2 + mod(c + dc, 2)
                k = t * 4 + dzl * 2 + dc
                copy = remote(att.at[source], att.at[source], o_s.at[k], o_r.at[k], y=up)
                copy.wait_recv()
                copy.wait_send()

    hidden = jnp.zeros((64, VIT_D), F32)
    for h in range(0, VIT_HEADS, 2):
        both = jnp.concatenate([att[h], att[h + 1]], axis=1)
        hidden += jnp.dot(
            both, wov[pl.ds(h, 2)].reshape(2 * HD, VIT_D), preferred_element_type=F32
        )
    hidden = jnp.where(live[...] > 0.0, hidden, 0.0)
    centred = hidden - jnp.mean(hidden, axis=1, keepdims=True)
    spread = jnp.mean(centred * centred, axis=1, keepdims=True)
    normed = (centred * lax.rsqrt(spread + 1e-6) * gain[...]).astype(BF16).astype(F32)
    for i in range(VIT_D // HD):
        nf[pl.ds(i * 64, 64), :] = normed[:, i * HD : (i + 1) * HD]

    lane = lax.broadcasted_iota(jnp.int32, (16, VIT_D), 1)
    quarter = [
        jnp.concatenate(
            [nf[pl.ds(i * 64 + j, 16, stride=4), :] for i in range(VIT_D // HD)], axis=1
        )
        for j in range(4)
    ]
    for part in range(4):
        out = jnp.zeros((16, VIT_D), F32)
        for j in range(4):
            for half in range(2):
                start = 320 * j + 160 * half
                origin = 640 * half + 160 * part
                shift = (start - origin) % VIT_D
                rolled = pltpu.roll(quarter[j], shift, 1) if shift else quarter[j]
                out = jnp.where((lane >= start) & (lane < start + 160), rolled, out)
        slab[part] = out.astype(BF16)
    for dy in range(1, 4):
        oy = mod(y + dy, 4)
        copy = remote(slab.at[oy], mid.at[y], m_s.at[dy], m_r.at[dy], y=oy)
        copy.start()
        sends.append(copy)
    mid[y] = slab[y]
    for dy in range(1, 4):
        source = mod(y + 4 - dy, 4)
        remote(mid.at[source], mid.at[source], m_s.at[dy], m_r.at[dy], y=up).wait_recv()

    right, left, far = mod(zh + 1, 4), mod(zh + 3, 4), mod(zh + 2, 4)
    oc = 1 - c
    mine = zh * 2 + c

    def pass_on(src, dst, k, **device):
        copy = remote(src, dst, t_s.at[k], t_r.at[k], **device)
        copy.start()
        sends.append(copy)

    def arrived(ref, k):
        remote(ref, ref, t_s.at[k], t_r.at[k], y=up).wait_recv()

    pass_on(mid, tok.at[mine], 0, zh=right)
    pass_on(mid, tok.at[mine], 1, zh=left)
    pass_on(mid, tok.at[mine], 2, c=oc)
    tok[mine] = mid[...]
    here = tok.at[left * 2 + c]
    arrived(here, 0)
    pass_on(here.at[pl.ds(0, 2)], here.at[pl.ds(0, 2)], 3, zh=right)
    pass_on(here, here, 4, c=oc)
    here = tok.at[right * 2 + c]
    arrived(here, 1)
    pass_on(here.at[pl.ds(2, 2)], here.at[pl.ds(2, 2)], 5, zh=left)
    pass_on(here, here, 6, c=oc)
    first, second = (tok.at[far * 2 + c].at[pl.ds(i, 2)] for i in (0, 2))
    arrived(first, 3)
    pass_on(first, first, 7, c=oc)
    arrived(second, 5)
    pass_on(second, second, 8, c=oc)
    arrived(tok.at[zh * 2 + oc], 2)
    arrived(tok.at[left * 2 + oc], 4)
    arrived(tok.at[right * 2 + oc], 6)
    arrived(tok.at[far * 2 + oc].at[pl.ds(0, 2)], 7)
    arrived(tok.at[far * 2 + oc].at[pl.ds(2, 2)], 8)
    for copy in sends:
        copy.wait_send()
    result = pltpu.make_async_copy(tok, tok_out, out_sem)
    result.start()
    result.wait()


def vit_tokens(packed, wo, gain, live):
    dma = pltpu.SemaphoreType.DMA
    vmem = pl.BlockSpec(memory_space=pltpu.VMEM)
    return pl.pallas_call(
        vit_kernel,
        out_shape=jax.ShapeDtypeStruct((8, 4, 16, VIT_D), BF16),
        in_specs=[vmem, pl.BlockSpec(memory_space=pl.ANY), vmem, vmem],
        out_specs=pl.BlockSpec(memory_space=pl.ANY),
        scratch_shapes=[
            pltpu.VMEM((4, 16, 64, PACKED), BF16),
            pltpu.VMEM((1024, PACKED), BF16),
            pltpu.VMEM((1024, PACKED), F32),
            pltpu.VMEM((1024, HD), F32),
            pltpu.VMEM((16, 64, HD), BF16),
            pltpu.VMEM((16, 64, HD), BF16),
            pltpu.VMEM((16, HD, VIT_D), BF16),
            pltpu.VMEM((64 * VIT_D // HD, HD), F32),
            pltpu.VMEM((4, 16, VIT_D), BF16),
            pltpu.VMEM((4, 16, VIT_D), BF16),
            pltpu.VMEM((8, 4, 16, VIT_D), BF16),
            dma((16,)), dma((16,)), dma((2, 16)), dma((2, 16)), dma((16,)), dma((16,)),
            dma((16,)), dma((16,)), dma((4,)), dma((4,)), dma((9,)), dma((9,)), dma((16,)), dma,
        ],
        compiler_params=pltpu.CompilerParams(collective_id=0, has_side_effects=True, vmem_limit_bytes=40 * 2**20),
        cost_estimate=pl.CostEstimate(flops=60_000_000_000, bytes_accessed=8_000_000, transcendentals=4_200_000),
        name="vit",
    )(packed, wo, gain, live)


def merge_kernel(
    tok, merger, kvw, gain, vis_out,
    mw, kw, sb, ra, rb, kvf, cs, cr, ks, ka, kb, ssr, vis,
    s_y, r_y, s_c, r_c, s_q, r_q, s_z, r_z, s_v, r_v, l_sem,
):
    y, zh, zl, c = (lax.axis_index(a) for a in ("y", "zh", "zl", "c"))
    up, down, across = mod(y + 1, 4), mod(y + 3, 4), mod(y + 2, 4)
    right, left, far = mod(zh + 1, 4), mod(zh + 3, 4), mod(zh + 2, 4)
    oc, ozl = 1 - c, 1 - zl
    load_m = pltpu.make_async_copy(merger, mw, l_sem.at[0])
    load_k = pltpu.make_async_copy(kvw, kw, l_sem.at[1])
    load_m.start()
    load_k.start()
    peers = [{"y": up}, {"y": down}, {"zl": ozl}]
    others = [(dzh, dc) for dzh in range(4) for dc in range(2) if dzh or dc]
    peers += [{"zh": mod(zh + dzh, 4), "c": mod(c + dc, 2)} for dzh, dc in others]
    meet(peers)
    sends = []

    def go(src, dst, ss, rs, **device):
        copy = remote(src, dst, ss, rs, **device)
        copy.start()
        sends.append(copy)

    def arrived(ref, ss, rs):
        remote(ref, ref, ss, rs, y=up).wait_recv()

    load_m.wait()

    def part(index):
        rows = pl.ds(pl.multiple_of(index * 128, 128), 128)
        return jnp.dot(tok[rows, :], mw[...], preferred_element_type=F32)

    sb[0] = part(across).astype(BF16)
    go(sb.at[0, pl.ds(0, 64)], ra.at[0], s_y.at[0], r_y.at[0], y=up)
    go(sb.at[0, pl.ds(64, 64)], ra.at[1], s_y.at[1], r_y.at[1], y=down)
    nxt, prv = part(up), part(down)
    arrived(ra.at[0], s_y.at[0], r_y.at[0])
    sb[1, 0:64] = (nxt[0:64] + ra[0].astype(F32)).astype(BF16)
    sb[1, 64:128] = nxt[64:128].astype(BF16)
    go(sb.at[1], rb.at[0], s_y.at[2], r_y.at[2], y=up)
    arrived(ra.at[1], s_y.at[1], r_y.at[1])
    sb[2, 0:64] = prv[0:64].astype(BF16)
    sb[2, 64:128] = (prv[64:128] + ra[1].astype(F32)).astype(BF16)
    go(sb.at[2], rb.at[1], s_y.at[3], r_y.at[3], y=down)
    own = part(y)
    arrived(rb.at[0], s_y.at[2], r_y.at[2])
    arrived(rb.at[1], s_y.at[3], r_y.at[3])
    embedded = (own + rb[0].astype(F32) + rb[1].astype(F32)).astype(BF16).astype(F32)
    square = jnp.sum(embedded * embedded, axis=1, keepdims=True)
    turned = jnp.transpose(jnp.broadcast_to(square, (128, 128)))
    ssr[zh * 2 + c] = turned[0:8]
    for k, (dzh, dc) in enumerate(others):
        slot = ssr.at[zh * 2 + c]
        go(slot, slot, s_q.at[k], r_q.at[k], zh=mod(zh + dzh, 4), c=mod(c + dc, 2))
    scaled = (embedded * gain[...]).astype(BF16)
    load_k.wait()
    for i in range(8):
        both = nt_dot(scaled, kw[pl.ds(i * 256, 256), :])
        kvf[2 * i] = both[:, :128]
        kvf[2 * i + 1] = both[:, 128:]

    for j in range(4):
        for k in range(2):
            cs[j, k] = kvf[k * 8 + j * 2 + oc].astype(BF16)
    go(cs, cr, s_c, r_c, c=oc)
    arrived(cr, s_c, r_c)

    def term(j, k):
        return kvf[k * 8 + j * 2 + c] + cr[j, k].astype(F32)

    for k in range(2):
        ks[0, k] = term(far, k).astype(BF16)
    go(ks.at[0, 0], ka.at[0], s_z.at[0], r_z.at[0], zh=right)
    go(ks.at[0, 1], ka.at[1], s_z.at[1], r_z.at[1], zh=left)
    arrived(ka.at[0], s_z.at[0], r_z.at[0])
    ks[1, 0] = (term(right, 0) + ka[0].astype(F32)).astype(BF16)
    ks[1, 1] = term(right, 1).astype(BF16)
    go(ks.at[1], kb.at[0], s_z.at[2], r_z.at[2], zh=right)
    arrived(ka.at[1], s_z.at[1], r_z.at[1])
    ks[2, 0] = term(left, 0).astype(BF16)
    ks[2, 1] = (term(left, 1) + ka[1].astype(F32)).astype(BF16)
    go(ks.at[2], kb.at[1], s_z.at[3], r_z.at[3], zh=left)
    for k, (dzh, dc) in enumerate(others):
        slot = ssr.at[mod(zh + 4 - dzh, 4) * 2 + mod(c + dc, 2)]
        arrived(slot, s_q.at[k], r_q.at[k])
    total = jnp.sum(ssr[...], axis=0)[0:1]
    factor = lax.rsqrt(jnp.broadcast_to(total, (128, 128)) / D + 1e-6)
    factor = jnp.transpose(factor)
    arrived(kb.at[0], s_z.at[2], r_z.at[2])
    arrived(kb.at[1], s_z.at[3], r_z.at[3])
    for k in range(2):
        done = term(zh, k) + kb[0, k].astype(F32) + kb[1, k].astype(F32)
        vis[y, zl, k] = (done * factor).astype(BF16)

    first = vis.at[y, zl]
    go(first, first, s_v.at[0], r_v.at[0], zl=ozl)
    go(first, first, s_v.at[1], r_v.at[1], y=up)
    go(first, first, s_v.at[2], r_v.at[2], y=down)
    second = vis.at[y, ozl]
    arrived(second, s_v.at[0], r_v.at[0])
    go(second, second, s_v.at[3], r_v.at[3], y=up)
    go(second, second, s_v.at[4], r_v.at[4], y=down)
    below = vis.at[down, zl]
    arrived(below, s_v.at[1], r_v.at[1])
    go(below, below, s_v.at[5], r_v.at[5], y=up)
    above = vis.at[up, ozl]
    arrived(above, s_v.at[4], r_v.at[4])
    go(above, above, s_v.at[6], r_v.at[6], y=down)
    arrived(vis.at[up, zl], s_v.at[2], r_v.at[2])
    arrived(vis.at[down, ozl], s_v.at[3], r_v.at[3])
    arrived(vis.at[across, zl], s_v.at[5], r_v.at[5])
    arrived(vis.at[across, ozl], s_v.at[6], r_v.at[6])
    for copy in sends:
        copy.wait_send()
    result = pltpu.make_async_copy(vis, vis_out, l_sem.at[2])
    result.start()
    result.wait()


def visual_keys_values(tok, merger, kvw, gain):
    dma = pltpu.SemaphoreType.DMA
    vmem = pl.BlockSpec(memory_space=pltpu.VMEM)
    hbm = pl.BlockSpec(memory_space=pl.ANY)
    return pl.pallas_call(
        merge_kernel,
        out_shape=jax.ShapeDtypeStruct((4, 2, 2, 128, 128), BF16),
        in_specs=[vmem, hbm, hbm, vmem],
        out_specs=hbm,
        scratch_shapes=[
            pltpu.VMEM((1280, 1024), BF16),
            pltpu.VMEM((2048, 1024), BF16),
            pltpu.VMEM((3, 128, 1024), BF16),
            pltpu.VMEM((2, 64, 1024), BF16),
            pltpu.VMEM((2, 128, 1024), BF16),
            pltpu.VMEM((16, 128, 128), F32),
            pltpu.VMEM((4, 2, 128, 128), BF16),
            pltpu.VMEM((4, 2, 128, 128), BF16),
            pltpu.VMEM((3, 2, 128, 128), BF16),
            pltpu.VMEM((2, 128, 128), BF16),
            pltpu.VMEM((2, 2, 128, 128), BF16),
            pltpu.VMEM((8, 8, 128), F32),
            pltpu.VMEM((4, 2, 2, 128, 128), BF16),
            dma((4,)), dma((4,)), dma, dma, dma((7,)), dma((7,)), dma((4,)), dma((4,)),
            dma((7,)), dma((7,)), dma((3,)),
        ],
        compiler_params=pltpu.CompilerParams(collective_id=1, has_side_effects=True, vmem_limit_bytes=40 * 2**20),
        cost_estimate=pl.CostEstimate(flops=20_000_000_000, bytes_accessed=8_000_000, transcendentals=0),
        name="merge",
    )(tok, merger, kvw, gain)


ROWS = 256


def lm_kernel(q, vis, span, bias, out):
    tile = pl.program_id(0)
    scale = HD**-0.5 * LOG2E
    ones = jnp.ones((1536, HD), BF16)
    keys = vis[:, :, 0].reshape(1024, HD)
    values = vis[:, :, 1].reshape(1024, HD)
    query = q[...]
    far = nt_dot(query, keys) + bias[...]
    near = nt_dot(query, span[0])
    token = (tile * ROWS + lax.broadcasted_iota(jnp.int32, (ROWS, 512), 0)) // 8
    place = lax.broadcasted_iota(jnp.int32, (ROWS, 512), 1)
    near = jnp.where(place <= token, near, MASKED)
    top = jnp.maximum(jnp.max(far, axis=1, keepdims=True), jnp.max(near, axis=1, keepdims=True))
    far = jnp.exp2((far - top) * scale).astype(BF16)
    near = jnp.exp2((near - top) * scale).astype(BF16)
    total = jnp.dot(
        far, jnp.concatenate([values, ones[:1024]], axis=1), preferred_element_type=F32
    ) + jnp.dot(near, jnp.concatenate([span[1], ones[:512]], axis=1), preferred_element_type=F32)
    out[...] = (total[:, :HD] / total[:, HD : HD + 1]).astype(BF16)


def lm_attention(q, vis, span, bias):
    whole = lambda *shape: pl.BlockSpec(shape, lambda i: (0,) * len(shape))
    rows = q.shape[0]
    return pl.pallas_call(
        lm_kernel,
        out_shape=jax.ShapeDtypeStruct((rows, HD), BF16),
        grid=(rows // ROWS,),
        in_specs=[
            pl.BlockSpec((ROWS, HD), lambda i: (i, 0)),
            whole(4, 2, 2, 128, 128),
            whole(2, 512, HD),
            whole(1, 1024),
        ],
        out_specs=pl.BlockSpec((ROWS, HD), lambda i: (i, 0)),
        compiler_params=pltpu.CompilerParams(vmem_limit_bytes=40 * 2**20),
        name="lm",
    )(q, vis, span, bias)


def pack_patches(vit_qkv, patch_total, first_patch):
    rows = vit_qkv.shape[1]
    split = vit_qkv[0].reshape(rows, 3, VIT_HEADS, VIT_HDIM).transpose(1, 2, 0, 3)
    ids = first_patch + jnp.arange(rows, dtype=jnp.int32)
    live = ids < patch_total
    mask = jnp.broadcast_to(
        jnp.where(live, 0.0, MASKED).astype(BF16)[None, :, None], (VIT_HEADS, rows, 1)
    )
    one = jnp.ones((VIT_HEADS, rows, 1), BF16)
    rest = jnp.zeros((VIT_HEADS, rows, PACKED - QUERY_AT - VIT_HDIM), BF16)
    packed = jnp.concatenate([split[2], one, mask, split[1], split[0], rest], axis=-1)
    return packed, live.astype(F32)[:, None]


def local(
    vit_qkv,
    patch_counts,
    vit_out_weight,
    vit_norm_gain,
    merger_weight,
    lm_norm_gain,
    kv_weight,
    queries,
    span_kv,
):
    patch_total = patch_counts[0]
    seq = lax.axis_index(SEQ)
    tp = lax.axis_index(TP)
    merger = lax.all_gather(merger_weight, ("x", "zl"), axis=0, tiled=True)
    kvw = lax.all_gather(kv_weight.T, IMG_SEQ, axis=0, tiled=True)
    packed, live = pack_patches(vit_qkv, patch_total, (seq * 8 + tp) * vit_qkv.shape[1])
    tok = vit_tokens(packed, vit_out_weight, vit_norm_gain[None], live)
    vis = visual_keys_values(tok.reshape(512, VIT_D), merger, kvw, lm_norm_gain[None])
    key = jnp.arange(1024, dtype=jnp.int32)
    block, r = key // 128, key % 128
    token = (((block % 2) * 4 + r // 16 % 4) * 8 + (block // 2) * 2 + r // 64) * 16 + r % 16
    bias = jnp.where(token < patch_total // 4, 0.0, MASKED)[None].astype(F32)
    rows = queries.shape[1] * queries.shape[2]
    span = span_kv[0, :, :, 0].transpose(1, 0, 2)
    out = lm_attention(queries.reshape(rows, HD), vis, span, bias)
    return out.reshape(queries.shape)


def solution(mesh):
    fine = Mesh(mesh.devices.reshape(4, 2, 4, 4, 2), ("x", "zl", "y", "zh", "c"))
    placed = (
        P("x", (*SEQ, *TP), None, None),
        P("x"),
        P(),
        P(),
        P(IMG_SEQ, TP),
        P(TP),
        P(TP, IMG_SEQ),
        P("x", SEQ, TP, None),
        P("x", SEQ, None, TP, None),
    )
    return jax.shard_map(
        local, mesh=fine, in_specs=placed, out_specs=P("x", SEQ, TP, None), check_vma=False
    )
```

time: 457 us -> 332 us (0.73)
  Pallas kernels: 0 us -> 144 us
  matrix products: 92.9 us -> 0 us
  blocking collectives: 56.2 us -> 0 us
  other arithmetic: 51.2 us -> 0.08 us
  local copies, waits for them, and re-layouts: 51.2 us -> 9.24 us
  starting transfers between devices: 22.6 us -> 0.04 us
    pallas_call x0 -> x3, Pallas kernels: none -> 144 us  [the longest x1 86.1 us: vit_tokens(): pl.pallas_call(vit_kernel, out_shape=jax.ShapeDtypeStruct((8, 4, 16, VIT_...]
    all_to_all x5 -> x0, waiting for transfers between devices: 96.3 us -> none  [the longest x3 84.3 us: sent_to_all(): return lax.all_to_all(copies, axis, split_axis=0, concat_axis=0, tiled=True)]
    all_gather x3 -> x2, waiting for transfers between devices: 64.2 us -> 159 us  [the longest x1 157 us: local(): kvw = lax.all_gather(kv_weight.T, IMG_SEQ, axis=0, tiled=True)]
    dot_general x37 -> x0, matrix products: 92.9 us -> none  [the longest x17 45.3 us: fold_block(): jnp.einsum(forms, weights.astype(jnp.bfloat16), value_block, preferred_el...]
    all_gather x2 -> x0, blocking collectives: 39.6 us -> none  [the longest x1 27 us: in_one_piece_2(): out = lax.all_gather(both, axis, axis=dim, tiled=True)]
    reduce_sum x21 -> x0, other arithmetic: 30 us -> none  [the longest x17 28.1 us: fold_block(): weight_sum = weight_sum * decay + jnp.sum(weights, axis=-1)]
    all_to_all x5 -> x0, starting transfers between devices: 22.5 us -> none  [the longest x3 13.3 us: sent_to_all(): return lax.all_to_all(copies, axis, split_axis=0, concat_axis=0, tiled=True)]
    all_to_all x1 -> x0, blocking collectives: 16.7 us -> none  [local(): lax.all_to_all(local_qkv, SEQ, split_axis=2, concat_axis=0, tiled=True)]
  transfers between devices with their start and end apart: 8 -> 2, of which waited for: 7 -> 2; matrix products, arithmetic and copies ran while one was open for 29% -> 1% of each run, Pallas kernels for 0% -> 26%
where the time goes in v1:
time: 332 us; the launch traced here: 328 us
  waiting for transfers between devices  160 us (48%)
  Pallas kernels  144 us (43%)
  between operations  14.2 us (4%)
  local copies, waits for them, and re-layouts  9.24 us (3%)
    all_gather x1, waiting for transfers between devices, local(): kvw = lax.all_gather(kv_weight.T, IMG_SEQ, axis=0, tiled=True)  157 us
    pallas_call x1, Pallas kernels, vit_tokens(): pl.pallas_call(vit_kernel, out_shape=jax.ShapeDtypeStruct((8, 4, 16, VIT_...  86.1 us
    pallas_call x1, Pallas kernels, visual_keys_values(): pl.pallas_call(merge_kernel, out_shape=jax.ShapeDtypeStruct((4, 2, 2, 128...  37.4 us
    pallas_call x1, Pallas kernels, lm_attention(): pl.pallas_call(lm_kernel, out_shape=jax.ShapeDtypeStruct((rows, HD), BF16...  20.3 us
  transfers between devices with their start and end apart: 2, of which 2 were waited for; matrix products, arithmetic and copies ran while one was open for 1% of the time, Pallas kernels for 26%

profile of v1, /device:TPU:8, one launch (start us, length us, event | category | flops | bytes accessed | tf_op | source)
XLA Modules:
  0.0 327.7 jit_solution(5637085483041629337)
XLA Ops:
  6.5 0.0 copy-start.6
  6.5 0.0 copy-start.5
  6.5 0.0 all-gather.3.cloned.1.call-start
  6.5 0.7 all-gather.3.cloned.1.call-update
  7.3 0.0 all-gather.5.cloned.1.call-start
  7.3 0.7 all-gather.5.cloned.1.call-update
  8.0 2.2 reshape_squeeze.3
  10.2 0.2 copy.18
  11.0 0.0 copy-done.6
  11.1 0.0 copy-done.5
  11.2 0.1 slice_bitcast_fusion
  11.2 0.1 broadcast_in_dim.39
  11.5 0.7 concatenate.3.packed
  12.2 0.1 compare_select_fusion.2.bias
  12.3 0.0 copy-start.2
  12.3 1.9 copy-done.2
  14.2 0.0 copy-start.4
  14.2 86.1 %vit.1 = bf16[8,4,16,1280]{3,2,1,0:T(8,128)(2,1)S(1)} custom-call(bf16[16,64,256]{2,1,0:T(8,128)(2,1)S(1)} %concatenate.3.packed, bf16[1280,1280]{1,0:T(8,128)(2,1)S(1)} %copy-done.2, f32[1,1280]{1,0:T(1,128)S(1)} %broadcast_in_dim.41.gain, f32[64,1]{1,0:T(8,128)S(1)} %fusion.live), custom_call_target="tpu_custom_call" | custom-call | flops 60000002048 | bytes 8000000 | tf_op jit(solution)/shard_map/vit/pallas_call | solution.py:289
  100.3 1.6 all-gather.3.cloned.1.call-done.merger
  102.0 157.3 %all-gather.5.cloned.1.call-done.kvw = bf16[2048,1024]{1,0:T(8,128)(2,1)} async-done(((bf16[64,1024]{1,0:T(8,128)(2,1)}), bf16[2048,1024]{1,0:T(8,128)(2,1)}) %all-gather.5.cloned.1.call-update) | async-done | bytes 4194320 | tf_op jit(solution)/shard_map/all_gather | solution.py:539
  259.3 0.0 copy-done.4
  259.3 0.0 copy-start.1
  259.3 2.2 copy-done.1
  261.5 0.0 copy-start.3
  261.5 1.7 copy-done.3
  263.2 0.0 copy-start
  263.2 37.4 %merge.1.vis = bf16[4,2,2,128,128]{4,3,2,1,0:T(8,128)(2,1)S(1)} custom-call(bf16[512,1280]{1,0:T(8,128)(2,1)S(1)} %bitcast.33, bf16[1280,1024]{1,0:T(8,128)(2,1)S(1)} %copy-done.3, bf16[2048,1024]{1,0:T(8,128)(2,1)S(1)} %copy-done.1, f32[1,1024]{1,0:T(1,128)S(1)} %bitcast.32), custom_call_target="tpu_custom_call" | custom-call | flops 20000000000 | bytes 8000000 | tf_op jit(solution)/shard_map/merge/pallas_call | solution.py:439
  300.6 0.0 copy-done
  300.6 20.3 %lm.1 = bf16[4096,128]{1,0:T(8,128)(2,1)} custom-call(bf16[4096,128]{1,0:T(8,128)(2,1)S(1)} %bitcast.30, bf16[4,2,2,128,128]{4,3,2,1,0:T(8,128)(2,1)S(1)} %merge.1.vis, bf16[2,512,128]{2,1,0:T(8,128)(2,1)S(1)} %bitcast.31, f32[1,1024]{1,0:T(1,128)S(1)} %compare_select_fusion.2.bias), custom_call_target="tpu_custom_call" | custom-call | tf_op jit(solution)/shard_map/lm/pallas_call | solution.py:494
  (6 shorter events, 0.2 us)
Async XLA Ops:
  6.5 4.5 %copy-start.6 = (f32[1280]{0:T(1024)S(1)}, f32[1280]{0:T(1024)}, u32[]{:S(2)}) copy-start(f32[1280]{0:T(1024)} %param.12) | copy-start | bytes 15364
  6.5 4.5 %copy-start.5 = (bf16[1,512,2,1,128]{4,2,3,1,0:T(2,128)(2,1)S(1)}, bf16[1,512,2,1,128]{4,2,3,1,0:T(2,128)(2,1)}, u32[]{:S(2)}) copy-start(bf16[1,512,2,1,128]{4,2,3,1,0:T(2,128)(2,1)} %param.17) | copy-start | bytes 786436
  6.5 95.4 %all-gather.3.cloned.1.call-start = ((), (), s32[]{:S(2)}) async-start(), calls=%async_computation | async-start | bytes 2949120 | tf_op jit(solution)/shard_map/all_gather | solution.py:538
  7.3 252.0 %all-gather.5.cloned.1.call-start = ((), (), s32[]{:S(2)}) async-start(), calls=%async_computation.1 | async-start | bytes 4325376 | tf_op jit(solution)/shard_map/all_gather | solution.py:539
  12.3 1.9 copy-start.2
  14.2 245.1 %copy-start.4 = (f32[1024]{0:T(1024)S(1)}, f32[1024]{0:T(1024)}, u32[]{:S(2)}) copy-start(f32[1024]{0:T(1024)} %param.14) | copy-start | bytes 12292
  259.3 2.2 copy-start.1
  261.5 1.7 copy-start.3
  263.2 37.4 %copy-start = (bf16[1,512,8,128]{3,2,1,0:T(8,128)(2,1)S(1)}, bf16[1,512,8,128]{3,2,1,0:T(8,128)(2,1)}, u32[]{:S(2)}) copy-start(bf16[1,512,8,128]{3,2,1,0:T(8,128)(2,1)} %param.16) | copy-start | bytes 3145732
Sparse Core Ops, SparseCore 0:
  9.1 92.7 all-gather.2
  103.7 155.5 all-gather.4

commit v2 on v1

v2 whole, which is shorter than its diff:
```python
import jax
import jax.numpy as jnp
from jax import lax
from jax.experimental import pallas as pl
from jax.experimental.pallas import tpu as pltpu
from jax.sharding import Mesh
from jax.sharding import PartitionSpec as P

VIT_D = 1280
VIT_HEADS = 16
VIT_HDIM = 80
D = 8192
HQ = 64
KVH = 8
HD = 128
SEQ = ("zl", "y")
TP = ("zh", "c")
IMG_SEQ = ("x", "zl", "y")
MASKED = -1e30
LOG2E = 1.4426950408889634
F32 = jnp.float32
BF16 = jnp.bfloat16

ONE_AT, MASK_AT, KEY_AT, QUERY_AT, PACKED = 80, 81, 82, 162, 256
RING_ORDER = (0, 1, 7, 2, 6, 3, 5, 4)


def remote(src, dst, send_sem, recv_sem, **device):
    return pltpu.make_async_remote_copy(
        src_ref=src,
        dst_ref=dst,
        send_sem=send_sem,
        recv_sem=recv_sem,
        device_id=device,
        device_id_type=pl.DeviceIdType.MESH,
    )


def mod(a, n):
    return lax.rem(a, n)


def meet(peers):
    barrier = pltpu.get_barrier_semaphore()
    for device in peers:
        pl.semaphore_signal(
            barrier, inc=1, device_id=device, device_id_type=pl.DeviceIdType.MESH
        )
    pl.semaphore_wait(barrier, len(peers))


def nt_dot(a, b):
    return lax.dot_general(a, b, (((1,), (1,)), ((), ())), preferred_element_type=F32)


def front_kernel(
    packed, wo, gain, live, merger, kvw, lm_gain, vis_out,
    kv, qp, acc, peak, back, att, wov, nf, slab, mid, tok,
    mw, kw0, kw1, sb, ra, rb, kvf, cs, cr, ks, ka, kb, ssr, vis,
    o_s, o_r, w_sem, sent, got,
):
    x, y, zh, zl, c = (lax.axis_index(a) for a in ("x", "y", "zh", "zl", "c"))
    z = zh * 2 + zl
    me = z * 2 + c
    up, down, across = mod(y + 1, 4), mod(y + 3, 4), mod(y + 2, 4)
    right, left, far = mod(zh + 1, 4), mod(zh + 3, 4), mod(zh + 2, 4)
    east, west, xfar = mod(x + 1, 4), mod(x + 3, 4), mod(x + 2, 4)
    oc, ozl = 1 - c, 1 - zl

    def place(dz, dc):
        other = mod(z + dz, 8)
        return other, mod(c + dc, 2)

    def device_of(other_z, other_c):
        return {"zh": lax.div(other_z, 2), "zl": mod(other_z, 2), "c": other_c}

    order = [(dz, dc) for dz in RING_ORDER for dc in range(2)]
    peers = [device_of(*place(dz, dc)) for dz, dc in order if (dz, dc) != (0, 0)]
    peers += [{"y": up}, {"y": down}, {"y": across}, {"x": east}, {"x": west}]
    meet(peers)

    numbers, sends = {}, []

    def number(name):
        return numbers.setdefault(name, len(numbers))

    def go(name, src, dst, **device):
        k = number(name)
        copy = remote(src, dst, sent.at[k], got.at[k], **device)
        copy.start()
        sends.append(copy)

    def arrived(name, ref):
        k = number(name)
        remote(ref, ref, sent.at[k], got.at[k], y=up).wait_recv()

    for dz in (4, 3, 5, 2, 6, 1, 7, 0):
        for dc in range(2):
            if (dz, dc) != (0, 0):
                oz, oc_ = place(dz, dc)
                go(("a", dz, dc), packed.at[oz * 2 + oc_], kv.at[y, me], **device_of(oz, oc_))
    weights = []
    for h in range(VIT_HEADS):
        copy = pltpu.make_async_copy(
            wo.at[pl.ds(h * VIT_HDIM, VIT_HDIM)], wov.at[h, pl.ds(0, VIT_HDIM)], w_sem.at[h]
        )
        copy.start()
        weights.append(copy)

    low, high = pl.ds(0, 32), pl.ds(32, 32)
    go(("w", "e", 0), merger, mw.at[x, zl], x=east)
    go(("w", "w", 0), merger, mw.at[x, zl], x=west)
    go(("w", "z"), merger, mw.at[x, zl], zl=ozl)
    go(("k0", "z"), kvw.at[low], kw0.at[y, x, zl], zl=ozl)
    go(("k1", "z"), kvw.at[high], kw1.at[x, y, zl], zl=ozl)
    go(("k0", "e", 0), kvw.at[low], kw0.at[y, x, zl], x=east)
    go(("k0", "w", 0), kvw.at[low], kw0.at[y, x, zl], x=west)
    kv[y, me] = packed[me]
    mw[x, zl] = merger[...]
    kw0[y, x, zl] = kvw[0:32]
    kw1[x, y, zl] = kvw[32:64]
    for h in range(VIT_HEADS):
        wov[h, VIT_HDIM:, :] = jnp.zeros((HD - VIT_HDIM, VIT_D), BF16)

    def source_of(dz, dc):
        return mod(z + 8 - dz, 8) * 2 + mod(c + dc, 2)

    for i, (dz, dc) in enumerate(order):
        source = source_of(dz, dc)
        if i == 0:
            block = packed.at[me]
        else:
            block = kv.at[y, source]
            arrived(("a", dz, dc), block)
        go(("y1", 0, i), block, kv.at[y, source], y=up)
        go(("y1", 1, i), block, kv.at[y, source], y=down)

    row = lax.broadcasted_iota(jnp.int32, (PACKED, PACKED), 0)
    col = lax.broadcasted_iota(jnp.int32, (PACKED, PACKED), 1)
    moved = (col >= KEY_AT) & (col < QUERY_AT) & (row == col + (QUERY_AT - KEY_AT))
    pick = moved | ((col == MASK_AT) & (row == ONE_AT))
    pick = jnp.where(pick, 1.0, 0.0).astype(BF16)
    scale = VIT_HDIM**-0.5 * LOG2E

    def fold(tile, slot, first):
        rows = pl.ds(pl.multiple_of(tile * 256, 256), 256)
        block = kv[slot].reshape(1024, PACKED)
        scores = nt_dot(qp[rows, :], block)
        top = jnp.max(scores, axis=1, keepdims=True)
        if first:
            weights = jnp.exp2((scores - top) * scale)
            total = jnp.dot(weights.astype(BF16), block, preferred_element_type=F32)
        else:
            old = peak[rows, :][:, :1]
            top = jnp.maximum(old, top)
            weights = jnp.exp2((scores - top) * scale)
            total = jnp.dot(weights.astype(BF16), block, preferred_element_type=F32)
            total += acc[rows, :] * jnp.exp2((old - top) * scale)
        peak[rows, :] = jnp.broadcast_to(top, (256, HD))
        return rows, total

    def whole(slot, first):
        def step(tile, carry):
            rows, total = fold(tile, slot, first)
            acc[rows, :] = total
            return carry

        lax.fori_loop(0, 4, step, 0)

    qp[...] = jnp.dot(
        kv[y].reshape(1024, PACKED), pick, preferred_element_type=F32
    ).astype(BF16)
    whole(y, True)

    arrived(("w", "z"), mw.at[x, ozl])
    go(("w", "e", 1), mw.at[x, ozl], mw.at[x, ozl], x=east)
    go(("w", "w", 1), mw.at[x, ozl], mw.at[x, ozl], x=west)
    arrived(("k0", "z"), kw0.at[y, x, ozl])
    go(("k0", "e", 1), kw0.at[y, x, ozl], kw0.at[y, x, ozl], x=east)
    go(("k0", "w", 1), kw0.at[y, x, ozl], kw0.at[y, x, ozl], x=west)

    for i, (dz, dc) in enumerate(order):
        way, origin, target = ((0, down, up), (1, up, down))[i % 2]
        block = kv.at[origin, source_of(dz, dc)]
        arrived(("y1", way, i), block)
        go(("y2", i), block, block, y=target)
    for i, (dz, dc) in enumerate(order):
        way, origin = ((1, up), (0, down))[i % 2]
        arrived(("y1", way, i), kv.at[origin, source_of(dz, dc)])

    arrived(("k1", "z"), kw1.at[x, y, ozl])
    go(("k1", "u", 0), kvw.at[high], kw1.at[x, y, zl], y=up)
    go(("k1", "d", 0), kvw.at[high], kw1.at[x, y, zl], y=down)
    go(("k1", "u", 1), kw1.at[x, y, ozl], kw1.at[x, y, ozl], y=up)
    go(("k1", "d", 1), kw1.at[x, y, ozl], kw1.at[x, y, ozl], y=down)
    whole(down, False)
    arrived(("w", "e", 0), mw.at[west, zl])
    go(("w", "e", 2), mw.at[west, zl], mw.at[west, zl], x=east)
    arrived(("k0", "e", 0), kw0.at[y, west, zl])
    go(("k0", "e", 2), kw0.at[y, west, zl], kw0.at[y, west, zl], x=east)
    whole(up, False)
    arrived(("w", "w", 1), mw.at[east, ozl])
    go(("w", "w", 2), mw.at[east, ozl], mw.at[east, ozl], x=west)
    arrived(("k0", "w", 1), kw0.at[y, east, ozl])
    go(("k0", "w", 2), kw0.at[y, east, ozl], kw0.at[y, east, ozl], x=west)
    for i, (dz, dc) in enumerate(order):
        arrived(("y2", i), kv.at[across, source_of(dz, dc)])

    def last(t, carry):
        tile = mod(zh + 1 + t, 4)
        _, total = fold(tile, across, False)
        done = (total[:, :HD] / total[:, ONE_AT : ONE_AT + 1]).astype(BF16)
        back[pl.ds(tile * 4, 4)] = done.reshape(4, 64, HD)
        for dzl in range(2):
            for dc in range(2):
                tzl, tc = mod(zl + dzl, 2), mod(c + dc, 2)
                k = t * 4 + dzl * 2 + dc
                copy = remote(
                    back.at[tile * 4 + tzl * 2 + tc], att.at[me], o_s.at[k], o_r.at[k],
                    zh=tile, zl=tzl, c=tc,
                )
                if dzl == 0 and dc == 0:
                    pl.when(t < 3)(copy.start)
                else:
                    copy.start()
        return carry

    lax.fori_loop(0, 4, last, 0)
    att[me] = back[me]

    arrived(("k1", "u", 0), kw1.at[x, down, zl])
    go(("k1", "u", 2), kw1.at[x, down, zl], kw1.at[x, down, zl], y=up)
    arrived(("k1", "d", 1), kw1.at[x, up, ozl])
    go(("k1", "d", 2), kw1.at[x, up, ozl], kw1.at[x, up, ozl], y=down)
    arrived(("k0", "w", 0), kw0.at[y, east, zl])
    arrived(("k0", "e", 1), kw0.at[y, west, ozl])
    arrived(("k0", "e", 2), kw0.at[y, xfar, zl])
    arrived(("k0", "w", 2), kw0.at[y, xfar, ozl])
    for copy in weights:
        copy.wait()
    for t in range(4):
        for dzl in range(2):
            for dc in range(2):
                if (t, dzl, dc) == (3, 0, 0):
                    continue
                source = mod(zh + 3 - t, 4) * 4 + mod(zl + dzl, 2) * 2 + mod(c + dc, 2)
                k = t * 4 + dzl * 2 + dc
                copy = remote(att.at[source], att.at[source], o_s.at[k], o_r.at[k], y=up)
                copy.wait_recv()
                copy.wait_send()
    go(("k0", "u"), kw0.at[y], kw0.at[y], y=up)
    go(("k0", "d"), kw0.at[y], kw0.at[y], y=down)

    hidden = jnp.zeros((64, VIT_D), F32)
    for h in range(0, VIT_HEADS, 2):
        both = jnp.concatenate([att[h], att[h + 1]], axis=1)
        hidden += jnp.dot(
            both, wov[pl.ds(h, 2)].reshape(2 * HD, VIT_D), preferred_element_type=F32
        )
    hidden = jnp.where(live[...] > 0.0, hidden, 0.0)
    centred = hidden - jnp.mean(hidden, axis=1, keepdims=True)
    spread = jnp.mean(centred * centred, axis=1, keepdims=True)
    normed = (centred * lax.rsqrt(spread + 1e-6) * gain[...]).astype(BF16).astype(F32)
    for i in range(VIT_D // HD):
        nf[pl.ds(i * 64, 64), :] = normed[:, i * HD : (i + 1) * HD]

    lane = lax.broadcasted_iota(jnp.int32, (16, VIT_D), 1)
    quarter = [
        jnp.concatenate(
            [nf[pl.ds(i * 64 + j, 16, stride=4), :] for i in range(VIT_D // HD)], axis=1
        )
        for j in range(4)
    ]
    for part in range(4):
        out = jnp.zeros((16, VIT_D), F32)
        for j in range(4):
            for half in range(2):
                start = 320 * j + 160 * half
                origin = 640 * half + 160 * part
                shift = (start - origin) % VIT_D
                rolled = pltpu.roll(quarter[j], shift, 1) if shift else quarter[j]
                out = jnp.where((lane >= start) & (lane < start + 160), rolled, out)
        slab[part] = out.astype(BF16)
    for dy in range(1, 4):
        oy = mod(y + dy, 4)
        go(("m", dy), slab.at[oy], mid.at[y], y=oy)
    mid[y] = slab[y]
    for dy in range(1, 4):
        arrived(("m", dy), mid.at[mod(y + 4 - dy, 4)])

    mine = zh * 2 + c
    go("t0", mid, tok.at[mine], zh=right)
    go("t1", mid, tok.at[mine], zh=left)
    go("t2", mid, tok.at[mine], c=oc)
    tok[mine] = mid[...]
    arrived(("k1", "d", 0), kw1.at[x, up, zl])
    arrived(("k1", "u", 1), kw1.at[x, down, ozl])
    arrived(("k1", "u", 2), kw1.at[x, across, zl])
    arrived(("k1", "d", 2), kw1.at[x, across, ozl])
    go(("k1", "e"), kw1.at[x], kw1.at[x], x=east)
    go(("k1", "w"), kw1.at[x], kw1.at[x], x=west)
    here = tok.at[left * 2 + c]
    arrived("t0", here)
    go("t3", here.at[pl.ds(0, 2)], here.at[pl.ds(0, 2)], zh=right)
    go("t4", here, here, c=oc)
    here = tok.at[right * 2 + c]
    arrived("t1", here)
    go("t5", here.at[pl.ds(2, 2)], here.at[pl.ds(2, 2)], zh=left)
    go("t6", here, here, c=oc)
    first, second = (tok.at[far * 2 + c].at[pl.ds(i, 2)] for i in (0, 2))
    arrived("t3", first)
    go("t7", first, first, c=oc)
    arrived("t5", second)
    go("t8", second, second, c=oc)
    arrived(("k0", "u"), kw0.at[down])
    go(("k0", "u", 2), kw0.at[down, pl.ds(0, 2)], kw0.at[down, pl.ds(0, 2)], y=up)
    arrived(("k0", "d"), kw0.at[up])
    go(("k0", "d", 2), kw0.at[up, pl.ds(2, 2)], kw0.at[up, pl.ds(2, 2)], y=down)
    arrived("t2", tok.at[zh * 2 + oc])
    arrived("t4", tok.at[left * 2 + oc])
    arrived("t6", tok.at[right * 2 + oc])
    arrived("t7", tok.at[far * 2 + oc].at[pl.ds(0, 2)])
    arrived("t8", tok.at[far * 2 + oc].at[pl.ds(2, 2)])
    arrived(("w", "w", 0), mw.at[east, zl])
    arrived(("w", "e", 1), mw.at[west, ozl])
    arrived(("w", "e", 2), mw.at[xfar, zl])
    arrived(("w", "w", 2), mw.at[xfar, ozl])

    def part(index):
        rows = tok[pl.ds(index * 2, 2)].reshape(128, VIT_D)
        return jnp.dot(rows, mw[...].reshape(VIT_D, 1024), preferred_element_type=F32)

    sb[0] = part(across).astype(BF16)
    go("s0", sb.at[0, pl.ds(0, 64)], ra.at[0], y=up)
    go("s1", sb.at[0, pl.ds(64, 64)], ra.at[1], y=down)
    nxt, prv = part(up), part(down)
    arrived("s0", ra.at[0])
    sb[1, 0:64] = (nxt[0:64] + ra[0].astype(F32)).astype(BF16)
    sb[1, 64:128] = nxt[64:128].astype(BF16)
    go("s2", sb.at[1], rb.at[0], y=up)
    arrived("s1", ra.at[1])
    sb[2, 0:64] = prv[0:64].astype(BF16)
    sb[2, 64:128] = (prv[64:128] + ra[1].astype(F32)).astype(BF16)
    go("s3", sb.at[2], rb.at[1], y=down)
    own = part(y)
    arrived(("k1", "e"), kw1.at[west])
    go(("k1", "e", 2), kw1.at[west, pl.ds(0, 2)], kw1.at[west, pl.ds(0, 2)], x=east)
    arrived(("k1", "w"), kw1.at[east])
    go(("k1", "w", 2), kw1.at[east, pl.ds(2, 2)], kw1.at[east, pl.ds(2, 2)], x=west)
    arrived("s2", rb.at[0])
    arrived("s3", rb.at[1])
    embedded = (own + rb[0].astype(F32) + rb[1].astype(F32)).astype(BF16).astype(F32)
    square = jnp.sum(embedded * embedded, axis=1, keepdims=True)
    turned = jnp.transpose(jnp.broadcast_to(square, (128, 128)))
    others = [(dzh, dc) for dzh in range(4) for dc in range(2) if dzh or dc]
    ssr[zh * 2 + c] = turned[0:8]
    for dzh, dc in others:
        slot = ssr.at[zh * 2 + c]
        go(("q", dzh, dc), slot, slot, zh=mod(zh + dzh, 4), c=mod(c + dc, 2))
    scaled = (embedded * lm_gain[...]).astype(BF16)
    arrived(("k0", "u", 2), kw0.at[across, pl.ds(0, 2)])
    arrived(("k0", "d", 2), kw0.at[across, pl.ds(2, 2)])
    arrived(("k1", "e", 2), kw1.at[xfar, pl.ds(0, 2)])
    arrived(("k1", "w", 2), kw1.at[xfar, pl.ds(2, 2)])

    def head_rows(k, t):
        kx, kz = 2 * k + t // 4, t % 4 // 2
        pieces = []
        for e in range(2):
            ky = 2 * (t % 2) + e
            pieces += [kw0[ky, kx, kz], kw1[kx, ky, kz]]
        return pieces

    for k in range(2):
        for t in range(0, 8, 2):
            both = jnp.concatenate(head_rows(k, t) + head_rows(k, t + 1), axis=0)
            both = nt_dot(scaled, both)
            kvf[k * 8 + t] = both[:, :128]
            kvf[k * 8 + t + 1] = both[:, 128:]

    for j in range(4):
        for k in range(2):
            cs[j, k] = kvf[k * 8 + j * 2 + oc].astype(BF16)
    go("c", cs, cr, c=oc)
    arrived("c", cr)

    def term(j, k):
        return kvf[k * 8 + j * 2 + c] + cr[j, k].astype(F32)

    for k in range(2):
        ks[0, k] = term(far, k).astype(BF16)
    go("z0", ks.at[0, 0], ka.at[0], zh=right)
    go("z1", ks.at[0, 1], ka.at[1], zh=left)
    arrived("z0", ka.at[0])
    ks[1, 0] = (term(right, 0) + ka[0].astype(F32)).astype(BF16)
    ks[1, 1] = term(right, 1).astype(BF16)
    go("z2", ks.at[1], kb.at[0], zh=right)
    arrived("z1", ka.at[1])
    ks[2, 0] = term(left, 0).astype(BF16)
    ks[2, 1] = (term(left, 1) + ka[1].astype(F32)).astype(BF16)
    go("z3", ks.at[2], kb.at[1], zh=left)
    for dzh, dc in others:
        arrived(("q", dzh, dc), ssr.at[mod(zh + 4 - dzh, 4) * 2 + mod(c + dc, 2)])
    total = jnp.sum(ssr[...], axis=0)[0:1]
    factor = lax.rsqrt(jnp.broadcast_to(total, (128, 128)) / D + 1e-6)
    factor = jnp.transpose(factor)
    arrived("z2", kb.at[0])
    arrived("z3", kb.at[1])
    for k in range(2):
        done = term(zh, k) + kb[0, k].astype(F32) + kb[1, k].astype(F32)
        vis[y, zl, k] = (done * factor).astype(BF16)

    first = vis.at[y, zl]
    go("v0", first, first, zl=ozl)
    go("v1", first, first, y=up)
    go("v2", first, first, y=down)
    second = vis.at[y, ozl]
    arrived("v0", second)
    go("v3", second, second, y=up)
    go("v4", second, second, y=down)
    below = vis.at[down, zl]
    arrived("v1", below)
    go("v5", below, below, y=up)
    above = vis.at[up, ozl]
    arrived("v4", above)
    go("v6", above, above, y=down)
    arrived("v2", vis.at[up, zl])
    arrived("v3", vis.at[down, ozl])
    arrived("v5", vis.at[across, zl])
    arrived("v6", vis.at[across, ozl])
    for copy in sends:
        copy.wait_send()
    result = pltpu.make_async_copy(vis, vis_out, w_sem.at[0])
    result.start()
    result.wait()


def visual_keys_values(packed, wo, gain, live, merger, kvw, lm_gain):
    dma = pltpu.SemaphoreType.DMA
    vmem = pl.BlockSpec(memory_space=pltpu.VMEM)
    hbm = pl.BlockSpec(memory_space=pl.ANY)
    return pl.pallas_call(
        front_kernel,
        out_shape=jax.ShapeDtypeStruct((4, 2, 2, 128, 128), BF16),
        in_specs=[vmem, hbm, vmem, vmem, vmem, vmem, vmem],
        out_specs=hbm,
        scratch_shapes=[
            pltpu.VMEM((4, 16, 64, PACKED), BF16),
            pltpu.VMEM((1024, PACKED), BF16),
            pltpu.VMEM((1024, PACKED), F32),
            pltpu.VMEM((1024, HD), F32),
            pltpu.VMEM((16, 64, HD), BF16),
            pltpu.VMEM((16, 64, HD), BF16),
            pltpu.VMEM((16, HD, VIT_D), BF16),
            pltpu.VMEM((64 * VIT_D // HD, HD), F32),
            pltpu.VMEM((4, 16, VIT_D), BF16),
            pltpu.VMEM((4, 16, VIT_D), BF16),
            pltpu.VMEM((8, 4, 16, VIT_D), BF16),
            pltpu.VMEM((4, 2, 160, 1024), BF16),
            pltpu.VMEM((4, 4, 2, 32, 1024), BF16),
            pltpu.VMEM((4, 4, 2, 32, 1024), BF16),
            pltpu.VMEM((3, 128, 1024), BF16),
            pltpu.VMEM((2, 64, 1024), BF16),
            pltpu.VMEM((2, 128, 1024), BF16),
            pltpu.VMEM((16, 128, 128), F32),
            pltpu.VMEM((4, 2, 128, 128), BF16),
            pltpu.VMEM((4, 2, 128, 128), BF16),
            pltpu.VMEM((3, 2, 128, 128), BF16),
            pltpu.VMEM((2, 128, 128), BF16),
            pltpu.VMEM((2, 2, 128, 128), BF16),
            pltpu.VMEM((8, 8, 128), F32),
            pltpu.VMEM((4, 2, 2, 128, 128), BF16),
            dma((16,)), dma((16,)), dma((16,)), dma((160,)), dma((160,)),
        ],
        compiler_params=pltpu.CompilerParams(
            collective_id=0, has_side_effects=True, vmem_limit_bytes=48 * 2**20
        ),
        cost_estimate=pl.CostEstimate(
            flops=60_000_000_000, bytes_accessed=8_000_000, transcendentals=4_200_000
        ),
        name="front",
    )(packed, wo, gain, live, merger, kvw, lm_gain)


ROWS = 256


def lm_kernel(q, vis, span, bias, out):
    tile = pl.program_id(0)
    scale = HD**-0.5 * LOG2E
    ones = jnp.ones((1536, HD), BF16)
    keys = vis[:, :, 0].reshape(1024, HD)
    values = vis[:, :, 1].reshape(1024, HD)
    query = q[...]
    far = nt_dot(query, keys) + bias[...]
    near = nt_dot(query, span[0])
    token = (tile * ROWS + lax.broadcasted_iota(jnp.int32, (ROWS, 512), 0)) // 8
    place = lax.broadcasted_iota(jnp.int32, (ROWS, 512), 1)
    near = jnp.where(place <= token, near, MASKED)
    top = jnp.maximum(jnp.max(far, axis=1, keepdims=True), jnp.max(near, axis=1, keepdims=True))
    far = jnp.exp2((far - top) * scale).astype(BF16)
    near = jnp.exp2((near - top) * scale).astype(BF16)
    total = jnp.dot(
        far, jnp.concatenate([values, ones[:1024]], axis=1), preferred_element_type=F32
    ) + jnp.dot(near, jnp.concatenate([span[1], ones[:512]], axis=1), preferred_element_type=F32)
    out[...] = (total[:, :HD] / total[:, HD : HD + 1]).astype(BF16)


def lm_attention(q, vis, span, bias):
    whole = lambda *shape: pl.BlockSpec(shape, lambda i: (0,) * len(shape))
    rows = q.shape[0]
    return pl.pallas_call(
        lm_kernel,
        out_shape=jax.ShapeDtypeStruct((rows, HD), BF16),
        grid=(rows // ROWS,),
        in_specs=[
            pl.BlockSpec((ROWS, HD), lambda i: (i, 0)),
            whole(4, 2, 2, 128, 128),
            whole(2, 512, HD),
            whole(1, 1024),
        ],
        out_specs=pl.BlockSpec((ROWS, HD), lambda i: (i, 0)),
        compiler_params=pltpu.CompilerParams(vmem_limit_bytes=40 * 2**20),
        name="lm",
    )(q, vis, span, bias)


def pack_patches(vit_qkv, patch_total, first_patch):
    rows = vit_qkv.shape[1]
    split = vit_qkv[0].reshape(rows, 3, VIT_HEADS, VIT_HDIM).transpose(1, 2, 0, 3)
    ids = first_patch + jnp.arange(rows, dtype=jnp.int32)
    live = ids < patch_total
    mask = jnp.broadcast_to(
        jnp.where(live, 0.0, MASKED).astype(BF16)[None, :, None], (VIT_HEADS, rows, 1)
    )
    one = jnp.ones((VIT_HEADS, rows, 1), BF16)
    rest = jnp.zeros((VIT_HEADS, rows, PACKED - QUERY_AT - VIT_HDIM), BF16)
    packed = jnp.concatenate([split[2], one, mask, split[1], split[0], rest], axis=-1)
    return packed, live.astype(F32)[:, None]


def local(
    vit_qkv,
    patch_counts,
    vit_out_weight,
    vit_norm_gain,
    merger_weight,
    lm_norm_gain,
    kv_weight,
    queries,
    span_kv,
):
    patch_total = patch_counts[0]
    seq = lax.axis_index(SEQ)
    tp = lax.axis_index(TP)
    packed, live = pack_patches(vit_qkv, patch_total, (seq * 8 + tp) * vit_qkv.shape[1])
    vis = visual_keys_values(
        packed, vit_out_weight, vit_norm_gain[None], live,
        merger_weight, kv_weight.T, lm_norm_gain[None],
    )
    key = jnp.arange(1024, dtype=jnp.int32)
    block, r = key // 128, key % 128
    token = (((block % 2) * 4 + r // 16 % 4) * 8 + (block // 2) * 2 + r // 64) * 16 + r % 16
    bias = jnp.where(token < patch_total // 4, 0.0, MASKED)[None].astype(F32)
    rows = queries.shape[1] * queries.shape[2]
    span = span_kv[0, :, :, 0].transpose(1, 0, 2)
    out = lm_attention(queries.reshape(rows, HD), vis, span, bias)
    return out.reshape(queries.shape)


def solution(mesh):
    fine = Mesh(mesh.devices.reshape(4, 2, 4, 4, 2), ("x", "zl", "y", "zh", "c"))
    placed = (
        P("x", (*SEQ, *TP), None, None),
        P("x"),
        P(),
        P(),
        P(IMG_SEQ, TP),
        P(TP),
        P(TP, IMG_SEQ),
        P("x", SEQ, TP, None),
        P("x", SEQ, None, TP, None),
    )
    return jax.shard_map(
        local, mesh=fine, in_specs=placed, out_specs=P("x", SEQ, TP, None), check_vma=False
    )
```

time: 332 us -> 152 us (0.46); the launches traced: 328 us -> 151 us
  waiting for transfers between devices: 160 us -> 0 us
  between operations: 14.2 us -> 0.87 us
  local copies, waits for them, and re-layouts: 9.24 us -> 5.33 us
    all_gather x2 -> x0, waiting for transfers between devices: 159 us -> none  [the longest x1 157 us: local(): kvw = lax.all_gather(kv_weight.T, IMG_SEQ, axis=0, tiled=True)]
    unnamed x15, local copies, waits for them, and re-layouts: 5.9 us -> 1.99 us
    pallas_call x2 -> x1, Pallas kernels: 123 us -> 125 us  [visual_keys_values(): pl.pallas_call(front_kernel, out_shape=jax.ShapeDtypeStruct((4, 2, 2, 128...]
  transfers between devices with their start and end apart: 2 -> 0, of which waited for: 2 -> 0; matrix products, arithmetic and copies ran while one was open for 1% -> 0% of each run, Pallas kernels for 26% -> 0%
where the time goes in v2:
time: 152 us; the launch traced here: 151 us
  Pallas kernels  145 us (95%)
  local copies, waits for them, and re-layouts  5.33 us (4%)
    pallas_call x1, Pallas kernels, visual_keys_values(): pl.pallas_call(front_kernel, out_shape=jax.ShapeDtypeStruct((4, 2, 2, 128...  125 us
    pallas_call x1, Pallas kernels, lm_attention(): pl.pallas_call(lm_kernel, out_shape=jax.ShapeDtypeStruct((rows, HD), BF16...  20.2 us

profile of v2, /device:TPU:8, one launch (start us, length us, event | category | flops | bytes accessed | tf_op | source)
XLA Modules:
  0.0 151.5 jit_solution(5225999662739259511)
XLA Ops:
  0.0 2.2 %reshape_squeeze.3 = bf16[64,3,16,80]{3,2,0,1:T(8,128)(2,1)S(1)} reshape(bf16[1,64,3,1280]{3,1,2,0:T(8,128)(2,1)} %param.9) | data formatting | bytes 983040 | tf_op jit(solution)/shard_map/reshape;squeeze | solution.py:530
  2.2 0.0 copy-start.6
  2.2 0.0 copy-start.2
  2.2 0.0 copy-start.3
  2.2 0.0 copy-start.4
  2.2 0.2 copy.18
  2.4 0.1 slice_bitcast_fusion
  3.2 0.1 broadcast_in_dim.39
  3.4 0.7 concatenate.3.packed
  4.1 0.0 copy-done.6
  4.1 0.0 copy-done.2
  4.2 0.0 copy-done.3
  4.2 0.0 copy-done.4
  4.2 0.0 copy-start.1
  4.2 1.9 %copy-done.1 = bf16[1280,1280]{1,0:T(8,128)(2,1)S(1)} copy-done((bf16[1280,1280]{1,0:T(8,128)(2,1)S(1)}, bf16[1280,1280]{1,0:T(8,128)(2,1)}, u32[]{:S(2)}) %copy-start.1) | copy-done | bytes 3276824
  6.1 0.0 copy-start.5
  6.1 0.0 copy-start
  6.1 125.0 %front.1.vis = bf16[4,2,2,128,128]{4,3,2,1,0:T(8,128)(2,1)S(1)} custom-call(bf16[16,64,256]{2,1,0:T(8,128)(2,1)S(1)} %concatenate.3.packed, bf16[1280,1280]{1,0:T(8,128)(2,1)S(1)} %copy-done.1, f32[1,1280]{1,0:T(1,128)S(1)} %broadcast_in_dim.41.gain, f32[64,1]{1,0:T(8,128)S(1)} %fusion.live, bf16[160,1024]{1,0:T(8,128)(2,1)S(1)} %copy-done.2, ...), custom_call_target="tpu_custom_call" | custom-call | flops 60000002048 | bytes 8000000 | tf_op jit(solution)/shard_map/front/pallas_call | solution.py:442
  131.1 0.0 copy-done.5
  131.2 0.1 compare_select_fusion.2.bias
  131.3 0.0 copy-done
  131.3 20.2 %lm.1 = bf16[4096,128]{1,0:T(8,128)(2,1)} custom-call(bf16[4096,128]{1,0:T(8,128)(2,1)S(1)} %bitcast.29, bf16[4,2,2,128,128]{4,3,2,1,0:T(8,128)(2,1)S(1)} %front.1.vis, bf16[2,512,128]{2,1,0:T(8,128)(2,1)S(1)} %bitcast.30, f32[1,1024]{1,0:T(1,128)S(1)} %compare_select_fusion.2.bias), custom_call_target="tpu_custom_call" | custom-call | tf_op jit(solution)/shard_map/lm/pallas_call | solution.py:512
  (6 shorter events, 0.2 us)
Async XLA Ops:
  2.2 1.9 %copy-start.6 = (f32[1280]{0:T(1024)S(1)}, f32[1280]{0:T(1024)}, u32[]{:S(2)}) copy-start(f32[1280]{0:T(1024)} %param.12) | copy-start | bytes 15364
  2.2 2.0 %copy-start.2 = (bf16[160,1024]{1,0:T(8,128)(2,1)S(1)}, bf16[160,1024]{1,0:T(8,128)(2,1)}, u32[]{:S(2)}) copy-start(bf16[160,1024]{1,0:T(8,128)(2,1)} %merger.1) | copy-start | bytes 983044
  2.2 2.0 %copy-start.3 = (bf16[1024,64]{0,1:T(8,128)(2,1)S(1)}, bf16[1024,64]{0,1:T(8,128)(2,1)}, u32[]{:S(2)}) copy-start(bf16[1024,64]{0,1:T(8,128)(2,1)} %param.15) | copy-start | bytes 393220
  2.2 2.0 %copy-start.4 = (f32[1024]{0:T(1024)S(1)}, f32[1024]{0:T(1024)}, u32[]{:S(2)}) copy-start(f32[1024]{0:T(1024)} %param.14) | copy-start | bytes 12292
  4.2 1.9 %copy-start.1 = (bf16[1280,1280]{1,0:T(8,128)(2,1)S(1)}, bf16[1280,1280]{1,0:T(8,128)(2,1)}, u32[]{:S(2)}) copy-start(bf16[1280,1280]{1,0:T(8,128)(2,1)} %wo.1) | copy-start | bytes 9830404
  6.1 125.0 %copy-start.5 = (bf16[1,512,2,1,128]{4,2,3,1,0:T(2,128)(2,1)S(1)}, bf16[1,512,2,1,128]{4,2,3,1,0:T(2,128)(2,1)}, u32[]{:S(2)}) copy-start(bf16[1,512,2,1,128]{4,2,3,1,0:T(2,128)(2,1)} %param.17) | copy-start | bytes 786436
  6.1 125.2 %copy-start = (bf16[1,512,8,128]{3,2,1,0:T(8,128)(2,1)S(1)}, bf16[1,512,8,128]{3,2,1,0:T(8,128)(2,1)}, u32[]{:S(2)}) copy-start(bf16[1,512,8,128]{3,2,1,0:T(8,128)(2,1)} %param.16) | copy-start | bytes 3145732

commit v3 on v2

--- a/solution.py
+++ b/solution.py
@@ -21,6 +21,7 @@
 F32 = jnp.float32
 BF16 = jnp.bfloat16
 
+LOW = 16
 ONE_AT, MASK_AT, KEY_AT, QUERY_AT, PACKED = 80, 81, 82, 162, 256
 RING_ORDER = (0, 1, 7, 2, 6, 3, 5, 4)
 
@@ -57,7 +58,7 @@
     packed, wo, gain, live, merger, kvw, lm_gain, vis_out,
     kv, qp, acc, peak, back, att, wov, nf, slab, mid, tok,
     mw, kw0, kw1, sb, ra, rb, kvf, cs, cr, ks, ka, kb, ssr, vis,
-    o_s, o_r, w_sem, sent, got,
+    w_sem, sent, got,
 ):
     x, y, zh, zl, c = (lax.axis_index(a) for a in ("x", "y", "zh", "zl", "c"))
     z = zh * 2 + zl
@@ -107,18 +108,18 @@
         copy.start()
         weights.append(copy)
 
-    low, high = pl.ds(0, 32), pl.ds(32, 32)
+    low, high = pl.ds(0, LOW), pl.ds(LOW, 64 - LOW)
+    go(("k0", "e", 0), kvw.at[low], kw0.at[y, x, zl], x=east)
+    go(("k0", "w", 0), kvw.at[low], kw0.at[y, x, zl], x=west)
     go(("w", "e", 0), merger, mw.at[x, zl], x=east)
     go(("w", "w", 0), merger, mw.at[x, zl], x=west)
-    go(("w", "z"), merger, mw.at[x, zl], zl=ozl)
     go(("k0", "z"), kvw.at[low], kw0.at[y, x, zl], zl=ozl)
     go(("k1", "z"), kvw.at[high], kw1.at[x, y, zl], zl=ozl)
-    go(("k0", "e", 0), kvw.at[low], kw0.at[y, x, zl], x=east)
-    go(("k0", "w", 0), kvw.at[low], kw0.at[y, x, zl], x=west)
+    go(("w", "z"), merger, mw.at[x, zl], zl=ozl)
     kv[y, me] = packed[me]
     mw[x, zl] = merger[...]
-    kw0[y, x, zl] = kvw[0:32]
-    kw1[x, y, zl] = kvw[32:64]
+    kw0[y, x, zl] = kvw[0:LOW]
+    kw1[x, y, zl] = kvw[LOW:64]
     for h in range(VIT_HEADS):
         wov[h, VIT_HDIM:, :] = jnp.zeros((HD - VIT_HDIM, VIT_D), BF16)
 
@@ -142,114 +143,107 @@
     pick = jnp.where(pick, 1.0, 0.0).astype(BF16)
     scale = VIT_HDIM**-0.5 * LOG2E
 
-    def fold(tile, slot, first):
-        rows = pl.ds(pl.multiple_of(tile * 256, 256), 256)
-        block = kv[slot].reshape(1024, PACKED)
+    def rows_of(tile):
+        return pl.ds(tile * 256 if isinstance(tile, int) else pl.multiple_of(tile * 256, 256), 256)
+
+    def score(tile, block, first):
+        rows = rows_of(tile)
         scores = nt_dot(qp[rows, :], block)
         top = jnp.max(scores, axis=1, keepdims=True)
         if first:
-            weights = jnp.exp2((scores - top) * scale)
-            total = jnp.dot(weights.astype(BF16), block, preferred_element_type=F32)
-        else:
-            old = peak[rows, :][:, :1]
-            top = jnp.maximum(old, top)
-            weights = jnp.exp2((scores - top) * scale)
-            total = jnp.dot(weights.astype(BF16), block, preferred_element_type=F32)
+            return scores, top, None
+        old = peak[rows, :][:, :1]
+        return scores, jnp.maximum(old, top), old
+
+    def blend(tile, block, scores, top, old):
+        rows = rows_of(tile)
+        weights = jnp.exp2((scores - top) * scale)
+        total = jnp.dot(weights.astype(BF16), block, preferred_element_type=F32)
+        if old is not None:
             total += acc[rows, :] * jnp.exp2((old - top) * scale)
         peak[rows, :] = jnp.broadcast_to(top, (256, HD))
-        return rows, total
-
-    def whole(slot, first):
-        def step(tile, carry):
-            rows, total = fold(tile, slot, first)
-            acc[rows, :] = total
-            return carry
-
-        lax.fori_loop(0, 4, step, 0)
+        return total
+
+    def whole(slot, first, tiles=(0, 1, 2, 3), store=None):
+        block = kv[slot].reshape(1024, PACKED)
+        ready = score(tiles[0], block, first)
+        for t, tile in enumerate(tiles):
+            following = score(tiles[t + 1], block, first) if t < 3 else None
+            total = blend(tile, block, *ready)
+            if store is None:
+                acc[rows_of(tile), :] = total
+            else:
+                store(t, tile, total)
+            ready = following
 
     qp[...] = jnp.dot(
         kv[y].reshape(1024, PACKED), pick, preferred_element_type=F32
     ).astype(BF16)
     whole(y, True)
 
-    arrived(("w", "z"), mw.at[x, ozl])
-    go(("w", "e", 1), mw.at[x, ozl], mw.at[x, ozl], x=east)
-    go(("w", "w", 1), mw.at[x, ozl], mw.at[x, ozl], x=west)
     arrived(("k0", "z"), kw0.at[y, x, ozl])
     go(("k0", "e", 1), kw0.at[y, x, ozl], kw0.at[y, x, ozl], x=east)
     go(("k0", "w", 1), kw0.at[y, x, ozl], kw0.at[y, x, ozl], x=west)
+    arrived(("k1", "z"), kw1.at[x, y, ozl])
+
+    def piece(row, k):
+        block = kw1.at[x, row]
+        go(("k1", "e", k), block, block, x=east)
+        go(("k1", "w", k), block, block, x=west)
+
+    piece(y, 0)
 
     for i, (dz, dc) in enumerate(order):
         way, origin, target = ((0, down, up), (1, up, down))[i % 2]
         block = kv.at[origin, source_of(dz, dc)]
         arrived(("y1", way, i), block)
         go(("y2", i), block, block, y=target)
+    go(("k1", "u"), kw1.at[x, y], kw1.at[x, y], y=up)
+    go(("k1", "d"), kw1.at[x, y], kw1.at[x, y], y=down)
     for i, (dz, dc) in enumerate(order):
         way, origin = ((1, up), (0, down))[i % 2]
         arrived(("y1", way, i), kv.at[origin, source_of(dz, dc)])
 
-    arrived(("k1", "z"), kw1.at[x, y, ozl])
-    go(("k1", "u", 0), kvw.at[high], kw1.at[x, y, zl], y=up)
-    go(("k1", "d", 0), kvw.at[high], kw1.at[x, y, zl], y=down)
-    go(("k1", "u", 1), kw1.at[x, y, ozl], kw1.at[x, y, ozl], y=up)
-    go(("k1", "d", 1), kw1.at[x, y, ozl], kw1.at[x, y, ozl], y=down)
     whole(down, False)
+    arrived(("w", "z"), mw.at[x, ozl])
+    go(("w", "e", 1), mw.at[x, ozl], mw.at[x, ozl], x=east)
+    go(("w", "w", 1), mw.at[x, ozl], mw.at[x, ozl], x=west)
+    arrived(("k0", "e", 0), kw0.at[y, west, zl])
+    go(("k0", "e", 2), kw0.at[y, west, zl], kw0.at[y, west, zl], x=east)
     arrived(("w", "e", 0), mw.at[west, zl])
     go(("w", "e", 2), mw.at[west, zl], mw.at[west, zl], x=east)
-    arrived(("k0", "e", 0), kw0.at[y, west, zl])
-    go(("k0", "e", 2), kw0.at[y, west, zl], kw0.at[y, west, zl], x=east)
     whole(up, False)
-    arrived(("w", "w", 1), mw.at[east, ozl])
-    go(("w", "w", 2), mw.at[east, ozl], mw.at[east, ozl], x=west)
     arrived(("k0", "w", 1), kw0.at[y, east, ozl])
     go(("k0", "w", 2), kw0.at[y, east, ozl], kw0.at[y, east, ozl], x=west)
     for i, (dz, dc) in enumerate(order):
         arrived(("y2", i), kv.at[across, source_of(dz, dc)])
 
-    def last(t, carry):
-        tile = mod(zh + 1 + t, 4)
-        _, total = fold(tile, across, False)
+    def give_back(t, tile, total):
         done = (total[:, :HD] / total[:, ONE_AT : ONE_AT + 1]).astype(BF16)
         back[pl.ds(tile * 4, 4)] = done.reshape(4, 64, HD)
         for dzl in range(2):
             for dc in range(2):
+                if (t, dzl, dc) == (3, 0, 0):
+                    continue
                 tzl, tc = mod(zl + dzl, 2), mod(c + dc, 2)
-                k = t * 4 + dzl * 2 + dc
-                copy = remote(
-                    back.at[tile * 4 + tzl * 2 + tc], att.at[me], o_s.at[k], o_r.at[k],
+                go(
+                    ("o", t, dzl, dc), back.at[tile * 4 + tzl * 2 + tc], att.at[me],
                     zh=tile, zl=tzl, c=tc,
                 )
-                if dzl == 0 and dc == 0:
-                    pl.when(t < 3)(copy.start)
-                else:
-                    copy.start()
-        return carry
-
-    lax.fori_loop(0, 4, last, 0)
+
+    whole(across, False, [mod(zh + 1 + t, 4) for t in range(4)], give_back)
     att[me] = back[me]
 
-    arrived(("k1", "u", 0), kw1.at[x, down, zl])
-    go(("k1", "u", 2), kw1.at[x, down, zl], kw1.at[x, down, zl], y=up)
-    arrived(("k1", "d", 1), kw1.at[x, up, ozl])
-    go(("k1", "d", 2), kw1.at[x, up, ozl], kw1.at[x, up, ozl], y=down)
-    arrived(("k0", "w", 0), kw0.at[y, east, zl])
-    arrived(("k0", "e", 1), kw0.at[y, west, ozl])
-    arrived(("k0", "e", 2), kw0.at[y, xfar, zl])
-    arrived(("k0", "w", 2), kw0.at[y, xfar, ozl])
+    arrived(("w", "w", 1), mw.at[east, ozl])
+    go(("w", "w", 2), mw.at[east, ozl], mw.at[east, ozl], x=west)
     for copy in weights:
         copy.wait()
     for t in range(4):
         for dzl in range(2):
             for dc in range(2):
-                if (t, dzl, dc) == (3, 0, 0):
-                    continue
-                source = mod(zh + 3 - t, 4) * 4 + mod(zl + dzl, 2) * 2 + mod(c + dc, 2)
-                k = t * 4 + dzl * 2 + dc
-                copy = remote(att.at[source], att.at[source], o_s.at[k], o_r.at[k], y=up)
-                copy.wait_recv()
-                copy.wait_send()
-    go(("k0", "u"), kw0.at[y], kw0.at[y], y=up)
-    go(("k0", "d"), kw0.at[y], kw0.at[y], y=down)
+                if (t, dzl, dc) != (3, 0, 0):
+                    source = mod(zh + 3 - t, 4) * 4 + mod(zl + dzl, 2) * 2 + mod(c + dc, 2)
+                    arrived(("o", t, dzl, dc), att.at[source])
 
     hidden = jnp.zeros((64, VIT_D), F32)
     for h in range(0, VIT_HEADS, 2):
@@ -285,6 +279,19 @@
         oy = mod(y + dy, 4)
         go(("m", dy), slab.at[oy], mid.at[y], y=oy)
     mid[y] = slab[y]
+
+    arrived(("k1", "u"), kw1.at[x, down])
+    go(("k1", "u", 2), kw1.at[x, down, 0], kw1.at[x, down, 0], y=up)
+    piece(down, 1)
+    arrived(("k1", "d"), kw1.at[x, up])
+    go(("k1", "d", 2), kw1.at[x, up, 1], kw1.at[x, up, 1], y=down)
+    piece(up, 2)
+    arrived(("k0", "w", 0), kw0.at[y, east, zl])
+    arrived(("k0", "e", 1), kw0.at[y, west, ozl])
+    arrived(("k0", "e", 2), kw0.at[y, xfar, zl])
+    arrived(("k0", "w", 2), kw0.at[y, xfar, ozl])
+    go(("k0", "u"), kw0.at[y], kw0.at[y], y=up)
+    go(("k0", "d"), kw0.at[y], kw0.at[y], y=down)
     for dy in range(1, 4):
         arrived(("m", dy), mid.at[mod(y + 4 - dy, 4)])
 
@@ -293,12 +300,19 @@
     go("t1", mid, tok.at[mine], zh=left)
     go("t2", mid, tok.at[mine], c=oc)
     tok[mine] = mid[...]
-    arrived(("k1", "d", 0), kw1.at[x, up, zl])
-    arrived(("k1", "u", 1), kw1.at[x, down, ozl])
-    arrived(("k1", "u", 2), kw1.at[x, across, zl])
-    arrived(("k1", "d", 2), kw1.at[x, across, ozl])
-    go(("k1", "e"), kw1.at[x], kw1.at[x], x=east)
-    go(("k1", "w"), kw1.at[x], kw1.at[x], x=west)
+    arrived(("k1", "u", 2), kw1.at[x, across, 0])
+    arrived(("k1", "d", 2), kw1.at[x, across, 1])
+    piece(across, 3)
+
+    def piece_on(k, row):
+        if k < 2:
+            block, way, target = kw1.at[west, row], "e", east
+        else:
+            block, way, target = kw1.at[east, row], "w", west
+        arrived(("k1", way, k), block)
+        go(("k1", way, k, 2), block, block, x=target)
+
+    piece_on(0, y)
     here = tok.at[left * 2 + c]
     arrived("t0", here)
     go("t3", here.at[pl.ds(0, 2)], here.at[pl.ds(0, 2)], zh=right)
@@ -312,6 +326,8 @@
     go("t7", first, first, c=oc)
     arrived("t5", second)
     go("t8", second, second, c=oc)
+    piece_on(1, down)
+    piece_on(2, up)
     arrived(("k0", "u"), kw0.at[down])
     go(("k0", "u", 2), kw0.at[down, pl.ds(0, 2)], kw0.at[down, pl.ds(0, 2)], y=up)
     arrived(("k0", "d"), kw0.at[up])
@@ -343,10 +359,7 @@
     sb[2, 64:128] = (prv[64:128] + ra[1].astype(F32)).astype(BF16)
     go("s3", sb.at[2], rb.at[1], y=down)
     own = part(y)
-    arrived(("k1", "e"), kw1.at[west])
-    go(("k1", "e", 2), kw1.at[west, pl.ds(0, 2)], kw1.at[west, pl.ds(0, 2)], x=east)
-    arrived(("k1", "w"), kw1.at[east])
-    go(("k1", "w", 2), kw1.at[east, pl.ds(2, 2)], kw1.at[east, pl.ds(2, 2)], x=west)
+    piece_on(3, across)
     arrived("s2", rb.at[0])
     arrived("s3", rb.at[1])
     embedded = (own + rb[0].astype(F32) + rb[1].astype(F32)).astype(BF16).astype(F32)
@@ -360,8 +373,13 @@
     scaled = (embedded * lm_gain[...]).astype(BF16)
     arrived(("k0", "u", 2), kw0.at[across, pl.ds(0, 2)])
     arrived(("k0", "d", 2), kw0.at[across, pl.ds(2, 2)])
-    arrived(("k1", "e", 2), kw1.at[xfar, pl.ds(0, 2)])
-    arrived(("k1", "w", 2), kw1.at[xfar, pl.ds(2, 2)])
+    for k, row in enumerate((y, down, up, across)):
+        if k < 2:
+            arrived(("k1", "w", k), kw1.at[east, row])
+            arrived(("k1", "e", k, 2), kw1.at[xfar, row])
+        else:
+            arrived(("k1", "e", k), kw1.at[west, row])
+            arrived(("k1", "w", k, 2), kw1.at[xfar, row])
 
     def head_rows(k, t):
         kx, kz = 2 * k + t // 4, t % 4 // 2
@@ -442,7 +460,7 @@
     return pl.pallas_call(
         front_kernel,
         out_shape=jax.ShapeDtypeStruct((4, 2, 2, 128, 128), BF16),
-        in_specs=[vmem, hbm, vmem, vmem, vmem, vmem, vmem],
+        in_specs=[vmem, pl.BlockSpec(memory_space=pltpu.HBM), vmem, vmem, vmem, vmem, vmem],
         out_specs=hbm,
         scratch_shapes=[
             pltpu.VMEM((4, 16, 64, PACKED), BF16),
@@ -457,8 +475,8 @@
             pltpu.VMEM((4, 16, VIT_D), BF16),
             pltpu.VMEM((8, 4, 16, VIT_D), BF16),
             pltpu.VMEM((4, 2, 160, 1024), BF16),
-            pltpu.VMEM((4, 4, 2, 32, 1024), BF16),
-            pltpu.VMEM((4, 4, 2, 32, 1024), BF16),
+            pltpu.VMEM((4, 4, 2, LOW, 1024), BF16),
+            pltpu.VMEM((4, 4, 2, 64 - LOW, 1024), BF16),
             pltpu.VMEM((3, 128, 1024), BF16),
             pltpu.VMEM((2, 64, 1024), BF16),
             pltpu.VMEM((2, 128, 1024), BF16),
@@ -470,7 +488,7 @@
             pltpu.VMEM((2, 2, 128, 128), BF16),
             pltpu.VMEM((8, 8, 128), F32),
             pltpu.VMEM((4, 2, 2, 128, 128), BF16),
-            dma((16,)), dma((16,)), dma((16,)), dma((160,)), dma((160,)),
+            dma((16,)), dma((192,)), dma((192,)),
         ],
         compiler_params=pltpu.CompilerParams(
             collective_id=0, has_side_effects=True, vmem_limit_bytes=48 * 2**20
@@ -482,28 +500,42 @@
     )(packed, wo, gain, live, merger, kvw, lm_gain)
 
 
-ROWS = 256
+ROWS = 1024
+TILE = 256
 
 
 def lm_kernel(q, vis, span, bias, out):
-    tile = pl.program_id(0)
+    step = pl.program_id(0)
     scale = HD**-0.5 * LOG2E
-    ones = jnp.ones((1536, HD), BF16)
     keys = vis[:, :, 0].reshape(1024, HD)
-    values = vis[:, :, 1].reshape(1024, HD)
-    query = q[...]
-    far = nt_dot(query, keys) + bias[...]
-    near = nt_dot(query, span[0])
-    token = (tile * ROWS + lax.broadcasted_iota(jnp.int32, (ROWS, 512), 0)) // 8
-    place = lax.broadcasted_iota(jnp.int32, (ROWS, 512), 1)
-    near = jnp.where(place <= token, near, MASKED)
-    top = jnp.maximum(jnp.max(far, axis=1, keepdims=True), jnp.max(near, axis=1, keepdims=True))
-    far = jnp.exp2((far - top) * scale).astype(BF16)
-    near = jnp.exp2((near - top) * scale).astype(BF16)
-    total = jnp.dot(
-        far, jnp.concatenate([values, ones[:1024]], axis=1), preferred_element_type=F32
-    ) + jnp.dot(near, jnp.concatenate([span[1], ones[:512]], axis=1), preferred_element_type=F32)
-    out[...] = (total[:, :HD] / total[:, HD : HD + 1]).astype(BF16)
+    ones = jnp.ones((1024, HD), BF16)
+    far_values = jnp.concatenate([vis[:, :, 1].reshape(1024, HD), ones], axis=1)
+    near_values = jnp.concatenate([span[1], ones[:512]], axis=1)
+    place = lax.broadcasted_iota(jnp.int32, (TILE, 512), 1)
+
+    def score(i):
+        query = q[pl.ds(i * TILE, TILE), :]
+        far = nt_dot(query, keys) + bias[...]
+        near = nt_dot(query, span[0])
+        row = lax.broadcasted_iota(jnp.int32, (TILE, 512), 0)
+        near = jnp.where(place <= (step * ROWS + i * TILE + row) // 8, near, MASKED)
+        top = jnp.maximum(
+            jnp.max(far, axis=1, keepdims=True), jnp.max(near, axis=1, keepdims=True)
+        )
+        return far, near, top
+
+    def blend(i, far, near, top):
+        far = jnp.exp2((far - top) * scale).astype(BF16)
+        near = jnp.exp2((near - top) * scale).astype(BF16)
+        total = jnp.dot(far, far_values, preferred_element_type=F32)
+        total += jnp.dot(near, near_values, preferred_element_type=F32)
+        out[pl.ds(i * TILE, TILE), :] = (total[:, :HD] / total[:, HD : HD + 1]).astype(BF16)
+
+    ready = score(0)
+    for i in range(ROWS // TILE):
+        following = score(i + 1) if i + 1 < ROWS // TILE else None
+        blend(i, *ready)
+        ready = following
 
 
 def lm_attention(q, vis, span, bias):

time: 152 us -> 127 us (0.84)
  Pallas kernels: 145 us -> 121 us
    pallas_call x1, Pallas kernels: 125 us -> 111 us  [visual_keys_values(): pl.pallas_call(front_kernel, out_shape=jax.ShapeDtypeStruct((4, 2, 2, 128...]
    pallas_call x1, Pallas kernels: 20.2 us -> 10.1 us  [lm_attention(): pl.pallas_call(lm_kernel, out_shape=jax.ShapeDtypeStruct((rows, HD), BF16...]
where the time goes in v3:
time: 127 us
  Pallas kernels  121 us (95%)
  local copies, waits for them, and re-layouts  5.33 us (4%)
    pallas_call x1, Pallas kernels, visual_keys_values(): pl.pallas_call(front_kernel, out_shape=jax.ShapeDtypeStruct((4, 2, 2, 128...  111 us
    pallas_call x1, Pallas kernels, lm_attention(): pl.pallas_call(lm_kernel, out_shape=jax.ShapeDtypeStruct((rows, HD), BF16...  10.1 us

profile of v3, /device:TPU:8, one launch (start us, length us, event | category | flops | bytes accessed | tf_op | source)
XLA Modules:
  0.0 127.0 jit_solution(11506439164551588027)
XLA Ops:
  0.0 2.2 %reshape_squeeze.3 = bf16[64,3,16,80]{3,2,0,1:T(8,128)(2,1)S(1)} reshape(bf16[1,64,3,1280]{3,1,2,0:T(8,128)(2,1)} %param.9) | data formatting | bytes 983040 | tf_op jit(solution)/shard_map/reshape;squeeze | solution.py:562
  2.2 0.0 copy-start.6
  2.2 0.0 copy-start.2
  2.2 0.0 copy-start.3
  2.2 0.0 copy-start.4
  2.2 0.2 copy.18
  2.4 0.1 slice_bitcast_fusion
  3.2 0.1 broadcast_in_dim.39
  3.4 0.7 concatenate.3.packed
  4.1 0.0 copy-done.6
  4.1 0.0 copy-done.2
  4.2 0.0 copy-done.3
  4.2 0.0 copy-done.4
  4.2 0.0 copy-start.1
  4.2 1.9 %copy-done.1 = bf16[1280,1280]{1,0:T(8,128)(2,1)S(1)} copy-done((bf16[1280,1280]{1,0:T(8,128)(2,1)S(1)}, bf16[1280,1280]{1,0:T(8,128)(2,1)}, u32[]{:S(2)}) %copy-start.1) | copy-done | bytes 3276824
  6.1 0.0 copy-start.5
  6.1 0.0 copy-start
  6.1 110.7 %front.1.vis = bf16[4,2,2,128,128]{4,3,2,1,0:T(8,128)(2,1)S(1)} custom-call(bf16[16,64,256]{2,1,0:T(8,128)(2,1)S(1)} %concatenate.3.packed, bf16[1280,1280]{1,0:T(8,128)(2,1)S(1)} %copy-done.1, f32[1,1280]{1,0:T(1,128)S(1)} %broadcast_in_dim.41.gain, f32[64,1]{1,0:T(8,128)S(1)} %fusion.live, bf16[160,1024]{1,0:T(8,128)(2,1)S(1)} %copy-done.2, ...), custom_call_target="tpu_custom_call" | custom-call | flops 60000002048 | bytes 8000000 | tf_op jit(solution)/shard_map/front/pallas_call | solution.py:460
  116.8 0.0 copy-done.5
  116.9 0.1 compare_select_fusion.2.bias
  116.9 0.0 copy-done
  116.9 10.1 %lm.1 = bf16[4096,128]{1,0:T(8,128)(2,1)} custom-call(bf16[4096,128]{1,0:T(8,128)(2,1)S(1)} %bitcast.29, bf16[4,2,2,128,128]{4,3,2,1,0:T(8,128)(2,1)S(1)} %front.1.vis, bf16[2,512,128]{2,1,0:T(8,128)(2,1)S(1)} %bitcast.30, f32[1,1024]{1,0:T(1,128)S(1)} %compare_select_fusion.2.bias), custom_call_target="tpu_custom_call" | custom-call | tf_op jit(solution)/shard_map/lm/pallas_call | solution.py:544
  (6 shorter events, 0.2 us)
Async XLA Ops:
  2.2 1.9 %copy-start.6 = (f32[1280]{0:T(1024)S(1)}, f32[1280]{0:T(1024)}, u32[]{:S(2)}) copy-start(f32[1280]{0:T(1024)} %param.12) | copy-start | bytes 15364
  2.2 2.0 %copy-start.2 = (bf16[160,1024]{1,0:T(8,128)(2,1)S(1)}, bf16[160,1024]{1,0:T(8,128)(2,1)}, u32[]{:S(2)}) copy-start(bf16[160,1024]{1,0:T(8,128)(2,1)} %merger.1) | copy-start | bytes 983044
  2.2 2.0 %copy-start.3 = (bf16[1024,64]{0,1:T(8,128)(2,1)S(1)}, bf16[1024,64]{0,1:T(8,128)(2,1)}, u32[]{:S(2)}) copy-start(bf16[1024,64]{0,1:T(8,128)(2,1)} %param.15) | copy-start | bytes 393220
  2.2 2.0 %copy-start.4 = (f32[1024]{0:T(1024)S(1)}, f32[1024]{0:T(1024)}, u32[]{:S(2)}) copy-start(f32[1024]{0:T(1024)} %param.14) | copy-start | bytes 12292
  4.2 1.9 %copy-start.1 = (bf16[1280,1280]{1,0:T(8,128)(2,1)S(1)}, bf16[1280,1280]{1,0:T(8,128)(2,1)}, u32[]{:S(2)}) copy-start(bf16[1280,1280]{1,0:T(8,128)(2,1)} %wo.1) | copy-start | bytes 9830404
  6.1 110.7 %copy-start.5 = (bf16[1,512,2,1,128]{4,2,3,1,0:T(2,128)(2,1)S(1)}, bf16[1,512,2,1,128]{4,2,3,1,0:T(2,128)(2,1)}, u32[]{:S(2)}) copy-start(bf16[1,512,2,1,128]{4,2,3,1,0:T(2,128)(2,1)} %param.17) | copy-start | bytes 786436
  6.1 110.8 %copy-start = (bf16[1,512,8,128]{3,2,1,0:T(8,128)(2,1)S(1)}, bf16[1,512,8,128]{3,2,1,0:T(8,128)(2,1)}, u32[]{:S(2)}) copy-start(bf16[1,512,8,128]{3,2,1,0:T(8,128)(2,1)} %param.16) | copy-start | bytes 3145732

commit v4 on v3

--- a/solution.py
+++ b/solution.py
@@ -22,6 +22,7 @@
 BF16 = jnp.bfloat16
 
 LOW = 16
+COPIES = 124
 ONE_AT, MASK_AT, KEY_AT, QUERY_AT, PACKED = 80, 81, 82, 162, 256
 RING_ORDER = (0, 1, 7, 2, 6, 3, 5, 4)
 
@@ -41,12 +42,13 @@
     return lax.rem(a, n)
 
 
-def meet(peers):
+def meet(peers, meanwhile):
     barrier = pltpu.get_barrier_semaphore()
     for device in peers:
         pl.semaphore_signal(
             barrier, inc=1, device_id=device, device_id_type=pl.DeviceIdType.MESH
         )
+    meanwhile()
     pl.semaphore_wait(barrier, len(peers))
 
 
@@ -55,9 +57,9 @@
 
 
 def front_kernel(
-    packed, wo, gain, live, merger, kvw, lm_gain, vis_out,
-    kv, qp, acc, peak, back, att, wov, nf, slab, mid, tok,
-    mw, kw0, kw1, sb, ra, rb, kvf, cs, cr, ks, ka, kb, ssr, vis,
+    counts, qkv, wo, gain, merger, kvw, lm_gain, queries, span, out,
+    packed, kv, qp, acc, peak, back, att, wov, nf, slab, mid, tok,
+    mw, kw0, kw1, sb, ra, rb, kvf, cs, cr, ks, ka, kb, ssr, vis, q, lacc, lpeak, result,
     w_sem, sent, got,
 ):
     x, y, zh, zl, c = (lax.axis_index(a) for a in ("x", "y", "zh", "zl", "c"))
@@ -78,28 +80,13 @@
     order = [(dz, dc) for dz in RING_ORDER for dc in range(2)]
     peers = [device_of(*place(dz, dc)) for dz, dc in order if (dz, dc) != (0, 0)]
     peers += [{"y": up}, {"y": down}, {"y": across}, {"x": east}, {"x": west}]
-    meet(peers)
-
-    numbers, sends = {}, []
-
-    def number(name):
-        return numbers.setdefault(name, len(numbers))
-
-    def go(name, src, dst, **device):
-        k = number(name)
-        copy = remote(src, dst, sent.at[k], got.at[k], **device)
-        copy.start()
-        sends.append(copy)
-
-    def arrived(name, ref):
-        k = number(name)
-        remote(ref, ref, sent.at[k], got.at[k], y=up).wait_recv()
-
-    for dz in (4, 3, 5, 2, 6, 1, 7, 0):
-        for dc in range(2):
-            if (dz, dc) != (0, 0):
-                oz, oc_ = place(dz, dc)
-                go(("a", dz, dc), packed.at[oz * 2 + oc_], kv.at[y, me], **device_of(oz, oc_))
+    total_patches = counts[0]
+    first_patch = ((zl * 4 + y) * 8 + zh * 2 + c) * 64
+    live = first_patch + lax.broadcasted_iota(jnp.int32, (64, PACKED), 0) < total_patches
+    low, high = pl.ds(0, LOW), pl.ds(LOW, 64 - LOW)
+
+    load_q = pltpu.make_async_copy(queries, q, w_sem.at[16])
+    load_q.start()
     weights = []
     for h in range(VIT_HEADS):
         copy = pltpu.make_async_copy(
@@ -108,34 +95,130 @@
         copy.start()
         weights.append(copy)
 
-    low, high = pl.ds(0, LOW), pl.ds(LOW, 64 - LOW)
+    def own_part():
+        column = lax.broadcasted_iota(jnp.int32, (64, PACKED), 1)
+        rest = jnp.where(column == ONE_AT, 1.0, 0.0)
+        rest = jnp.where((column == MASK_AT) & ~live, MASKED, rest)
+        for h in range(VIT_HEADS):
+            start = min(h * VIT_HDIM // HD * HD, VIT_D - PACKED)
+            row = rest
+            for which, at in ((2, 0), (1, KEY_AT), (0, QUERY_AT)):
+                window = qkv[which, :, start : start + PACKED].astype(F32)
+                shift = (at - (h * VIT_HDIM - start)) % PACKED
+                if shift:
+                    window = pltpu.roll(window, shift, 1)
+                row = jnp.where((column >= at) & (column < at + VIT_HDIM), window, row)
+            packed[h] = row.astype(BF16)
+        kv[y, me] = packed[me]
+        mw[x, zl] = merger[...]
+        kw0[y, x, zl] = kvw[0:LOW]
+        kw1[x, y, zl] = kvw[LOW:64]
+        for h in range(VIT_HEADS):
+            wov[h, VIT_HDIM:, :] = jnp.zeros((HD - VIT_HDIM, VIT_D), BF16)
+
+    meet(peers, own_part)
+
+    numbers, sends = {}, []
+
+    def number(name):
+        return numbers.setdefault(name, len(numbers))
+
+    def go(name, src, dst, **device):
+        k = number(name)
+        copy = remote(src, dst, sent.at[k], got.at[k], **device)
+        copy.start()
+        sends.append(copy)
+
+    def arrived(name, ref):
+        k = number(name)
+        remote(ref, ref, sent.at[k], got.at[k], y=up).wait_recv()
+
+    lm_scale = HD**-0.5 * LOG2E
+    lm_tiles = queries.shape[0] // 256
+
+    def lm_rows(i):
+        return pl.ds(i * 256, 256)
+
+    def near_part():
+        def near_score(i):
+            extent = (i // 4 + 1) * 128
+            keys = span[0, 0:extent, :]
+            scores = nt_dot(q[lm_rows(i), :], keys)
+            row = lax.broadcasted_iota(jnp.int32, (256, 128), 0)
+            place_ = lax.broadcasted_iota(jnp.int32, (256, 128), 1)
+            edge = jnp.where(
+                place_ + (extent - 128) <= (i * 256 + row) // 8, scores[:, extent - 128 :], MASKED
+            )
+            if extent > 128:
+                edge = jnp.concatenate([scores[:, : extent - 128], edge], axis=1)
+            return edge, jnp.max(edge, axis=1, keepdims=True), extent
+
+        ready = near_score(0)
+        for i in range(lm_tiles):
+            following = near_score(i + 1) if i + 1 < lm_tiles else None
+            scores, top, extent = ready
+            weights = jnp.exp2((scores - top) * lm_scale).astype(BF16)
+            values = jnp.concatenate([span[1, 0:extent, :], jnp.ones((extent, HD), BF16)], axis=1)
+            lacc[lm_rows(i), :] = jnp.dot(weights, values, preferred_element_type=F32)
+            lpeak[lm_rows(i), :] = jnp.broadcast_to(top, (256, HD))
+            ready = following
+
+    def far_part(slots, store, between):
+        keys = jnp.concatenate([vis[a, b, 0] for a, b in slots], axis=0)
+        values = jnp.concatenate([vis[a, b, 1] for a, b in slots], axis=0)
+        values = jnp.concatenate([values, jnp.ones((len(slots) * 128, HD), BF16)], axis=1)
+        lane = lax.broadcasted_iota(jnp.int32, (1, HD), 1)
+
+        def slot_bias(a, b):
+            patch = ((b * 4 + (lane >> 4 & 3)) * 8 + a * 2 + (lane >> 6)) * 64 + (lane & 15) * 4
+            return jnp.where(patch < total_patches, 0.0, MASKED)
+
+        shift = jnp.concatenate([slot_bias(a, b) for a, b in slots], axis=1)
+
+        def far_score(i):
+            scores = nt_dot(q[lm_rows(i), :], keys) + shift
+            old = lpeak[lm_rows(i), :]
+            return scores, jnp.maximum(old, jnp.max(scores, axis=1, keepdims=True)), old
+
+        ready = far_score(0)
+        for i in range(lm_tiles):
+            following = far_score(i + 1) if i + 1 < lm_tiles else None
+            scores, top, old = ready
+            spread = jnp.concatenate([top] * len(slots), axis=1)
+            weights = jnp.exp2((scores - spread) * lm_scale).astype(BF16)
+            total = jnp.dot(weights, values, preferred_element_type=F32)
+            fade = jnp.exp2((old - top) * lm_scale)
+            total += lacc[lm_rows(i), :] * jnp.concatenate([fade, fade], axis=1)
+            store(i, total, top)
+            between(i)
+            ready = following
+
+    for dz in (4, 3, 5, 2, 6, 1, 7, 0):
+        for dc in range(2):
+            if (dz, dc) != (0, 0):
+                oz, oc_ = place(dz, dc)
+                go(("a", dz, dc), packed.at[oz * 2 + oc_], kv.at[y, me], **device_of(oz, oc_))
     go(("k0", "e", 0), kvw.at[low], kw0.at[y, x, zl], x=east)
     go(("k0", "w", 0), kvw.at[low], kw0.at[y, x, zl], x=west)
     go(("w", "e", 0), merger, mw.at[x, zl], x=east)
     go(("w", "w", 0), merger, mw.at[x, zl], x=west)
+    def blocks_of(row, dz):
+        return kv.at[row, pl.ds(mod(z + 8 - dz, 8) * 2, 2)]
+
+    def source_of(dz, dc):
+        return mod(z + 8 - dz, 8) * 2 + mod(c + dc, 2)
+
+    for i, dz in enumerate(RING_ORDER):
+        for dc in range(2):
+            if (dz, dc) != (0, 0):
+                arrived(("a", dz, dc), kv.at[y, source_of(dz, dc)])
+        blocks = blocks_of(y, dz)
+        go(("y1", 0, i), blocks, blocks, y=up)
+        go(("y1", 1, i), blocks, blocks, y=down)
+
     go(("k0", "z"), kvw.at[low], kw0.at[y, x, zl], zl=ozl)
     go(("k1", "z"), kvw.at[high], kw1.at[x, y, zl], zl=ozl)
     go(("w", "z"), merger, mw.at[x, zl], zl=ozl)
-    kv[y, me] = packed[me]
-    mw[x, zl] = merger[...]
-    kw0[y, x, zl] = kvw[0:LOW]
-    kw1[x, y, zl] = kvw[LOW:64]
-    for h in range(VIT_HEADS):
-        wov[h, VIT_HDIM:, :] = jnp.zeros((HD - VIT_HDIM, VIT_D), BF16)
-
-    def source_of(dz, dc):
-        return mod(z + 8 - dz, 8) * 2 + mod(c + dc, 2)
-
-    for i, (dz, dc) in enumerate(order):
-        source = source_of(dz, dc)
-        if i == 0:
-            block = packed.at[me]
-        else:
-            block = kv.at[y, source]
-            arrived(("a", dz, dc), block)
-        go(("y1", 0, i), block, kv.at[y, source], y=up)
-        go(("y1", 1, i), block, kv.at[y, source], y=down)
-
     row = lax.broadcasted_iota(jnp.int32, (PACKED, PACKED), 0)
     col = lax.broadcasted_iota(jnp.int32, (PACKED, PACKED), 1)
     moved = (col >= KEY_AT) & (col < QUERY_AT) & (row == col + (QUERY_AT - KEY_AT))
@@ -149,19 +232,20 @@
     def score(tile, block, first):
         rows = rows_of(tile)
         scores = nt_dot(qp[rows, :], block)
-        top = jnp.max(scores, axis=1, keepdims=True)
+        top = jnp.broadcast_to(jnp.max(scores, axis=1, keepdims=True), (256, HD))
         if first:
             return scores, top, None
-        old = peak[rows, :][:, :1]
+        old = peak[rows, :]
         return scores, jnp.maximum(old, top), old
 
     def blend(tile, block, scores, top, old):
         rows = rows_of(tile)
-        weights = jnp.exp2((scores - top) * scale)
+        weights = jnp.exp2((scores - jnp.concatenate([top] * 8, axis=1)) * scale)
         total = jnp.dot(weights.astype(BF16), block, preferred_element_type=F32)
         if old is not None:
-            total += acc[rows, :] * jnp.exp2((old - top) * scale)
-        peak[rows, :] = jnp.broadcast_to(top, (256, HD))
+            fade = jnp.exp2((old - top) * scale)
+            total += acc[rows, :] * jnp.concatenate([fade, fade], axis=1)
+        peak[rows, :] = top
         return total
 
     def whole(slot, first, tiles=(0, 1, 2, 3), store=None):
@@ -181,6 +265,11 @@
     ).astype(BF16)
     whole(y, True)
 
+    for i, dz in enumerate(RING_ORDER):
+        way, origin, target = ((0, down, up), (1, up, down))[i % 2]
+        blocks = blocks_of(origin, dz)
+        arrived(("y1", way, i), blocks)
+        go(("y2", i), blocks, blocks, y=target)
     arrived(("k0", "z"), kw0.at[y, x, ozl])
     go(("k0", "e", 1), kw0.at[y, x, ozl], kw0.at[y, x, ozl], x=east)
     go(("k0", "w", 1), kw0.at[y, x, ozl], kw0.at[y, x, ozl], x=west)
@@ -193,16 +282,11 @@
 
     piece(y, 0)
 
-    for i, (dz, dc) in enumerate(order):
-        way, origin, target = ((0, down, up), (1, up, down))[i % 2]
-        block = kv.at[origin, source_of(dz, dc)]
-        arrived(("y1", way, i), block)
-        go(("y2", i), block, block, y=target)
     go(("k1", "u"), kw1.at[x, y], kw1.at[x, y], y=up)
     go(("k1", "d"), kw1.at[x, y], kw1.at[x, y], y=down)
-    for i, (dz, dc) in enumerate(order):
+    for i, dz in enumerate(RING_ORDER):
         way, origin = ((1, up), (0, down))[i % 2]
-        arrived(("y1", way, i), kv.at[origin, source_of(dz, dc)])
+        arrived(("y1", way, i), blocks_of(origin, dz))
 
     whole(down, False)
     arrived(("w", "z"), mw.at[x, ozl])
@@ -215,8 +299,8 @@
     whole(up, False)
     arrived(("k0", "w", 1), kw0.at[y, east, ozl])
     go(("k0", "w", 2), kw0.at[y, east, ozl], kw0.at[y, east, ozl], x=west)
-    for i, (dz, dc) in enumerate(order):
-        arrived(("y2", i), kv.at[across, source_of(dz, dc)])
+    for i, dz in enumerate(RING_ORDER):
+        arrived(("y2", i), blocks_of(across, dz))
 
     def give_back(t, tile, total):
         done = (total[:, :HD] / total[:, ONE_AT : ONE_AT + 1]).astype(BF16)
@@ -234,8 +318,6 @@
     whole(across, False, [mod(zh + 1 + t, 4) for t in range(4)], give_back)
     att[me] = back[me]
 
-    arrived(("w", "w", 1), mw.at[east, ozl])
-    go(("w", "w", 2), mw.at[east, ozl], mw.at[east, ozl], x=west)
     for copy in weights:
         copy.wait()
     for t in range(4):
@@ -251,7 +333,7 @@
         hidden += jnp.dot(
             both, wov[pl.ds(h, 2)].reshape(2 * HD, VIT_D), preferred_element_type=F32
         )
-    hidden = jnp.where(live[...] > 0.0, hidden, 0.0)
+    hidden = jnp.where(live[:, :1], hidden, 0.0)
     centred = hidden - jnp.mean(hidden, axis=1, keepdims=True)
     spread = jnp.mean(centred * centred, axis=1, keepdims=True)
     normed = (centred * lax.rsqrt(spread + 1e-6) * gain[...]).astype(BF16).astype(F32)
@@ -266,20 +348,22 @@
         for j in range(4)
     ]
     for part in range(4):
-        out = jnp.zeros((16, VIT_D), F32)
+        laid = jnp.zeros((16, VIT_D), F32)
         for j in range(4):
             for half in range(2):
                 start = 320 * j + 160 * half
                 origin = 640 * half + 160 * part
                 shift = (start - origin) % VIT_D
                 rolled = pltpu.roll(quarter[j], shift, 1) if shift else quarter[j]
-                out = jnp.where((lane >= start) & (lane < start + 160), rolled, out)
-        slab[part] = out.astype(BF16)
+                laid = jnp.where((lane >= start) & (lane < start + 160), rolled, laid)
+        slab[part] = laid.astype(BF16)
     for dy in range(1, 4):
         oy = mod(y + dy, 4)
         go(("m", dy), slab.at[oy], mid.at[y], y=oy)
     mid[y] = slab[y]
 
+    arrived(("w", "w", 1), mw.at[east, ozl])
+    go(("w", "w", 2), mw.at[east, ozl], mw.at[east, ozl], x=west)
     arrived(("k1", "u"), kw1.at[x, down])
     go(("k1", "u", 2), kw1.at[x, down, 0], kw1.at[x, down, 0], y=up)
     piece(down, 1)
@@ -300,6 +384,8 @@
     go("t1", mid, tok.at[mine], zh=left)
     go("t2", mid, tok.at[mine], c=oc)
     tok[mine] = mid[...]
+    load_q.wait()
+    near_part()
     arrived(("k1", "u", 2), kw1.at[x, across, 0])
     arrived(("k1", "d", 2), kw1.at[x, across, 1])
     piece(across, 3)
@@ -439,30 +525,55 @@
     below = vis.at[down, zl]
     arrived("v1", below)
     go("v5", below, below, y=up)
-    above = vis.at[up, ozl]
-    arrived("v4", above)
-    go("v6", above, above, y=down)
     arrived("v2", vis.at[up, zl])
+
+    def keep(i, total, top):
+        lacc[lm_rows(i), :] = total
+        lpeak[lm_rows(i), :] = top
+
+    def pass_up(i):
+        if i == 3:
+            above = vis.at[up, ozl]
+            arrived("v4", above)
+            go("v6", above, above, y=down)
+
+    far_part([(y, zl), (y, ozl), (down, zl), (up, zl)], keep, pass_up)
     arrived("v3", vis.at[down, ozl])
     arrived("v5", vis.at[across, zl])
     arrived("v6", vis.at[across, ozl])
+    stores = []
+
+    def finish(i, total, top):
+        result[lm_rows(i), :] = (total[:, :HD] / total[:, HD:]).astype(BF16)
+
+    def write(i):
+        if i % 4 == 3:
+            rows = pl.ds((i - 3) * 256, 1024)
+            copy = pltpu.make_async_copy(result.at[rows], out.at[rows], w_sem.at[17 + i // 4])
+            copy.start()
+            stores.append(copy)
+
+    far_part([(down, ozl), (up, ozl), (across, zl), (across, ozl)], finish, write)
+    assert len(numbers) == COPIES, len(numbers)
     for copy in sends:
         copy.wait_send()
-    result = pltpu.make_async_copy(vis, vis_out, w_sem.at[0])
-    result.start()
-    result.wait()
-
-
-def visual_keys_values(packed, wo, gain, live, merger, kvw, lm_gain):
+    for copy in stores:
+        copy.wait()
+
+
+def attend(counts, qkv, wo, gain, merger, kvw, lm_gain, queries, span):
     dma = pltpu.SemaphoreType.DMA
     vmem = pl.BlockSpec(memory_space=pltpu.VMEM)
     hbm = pl.BlockSpec(memory_space=pl.ANY)
     return pl.pallas_call(
         front_kernel,
-        out_shape=jax.ShapeDtypeStruct((4, 2, 2, 128, 128), BF16),
-        in_specs=[vmem, pl.BlockSpec(memory_space=pltpu.HBM), vmem, vmem, vmem, vmem, vmem],
+        out_shape=jax.ShapeDtypeStruct(queries.shape, BF16),
+        in_specs=[
+            pl.BlockSpec(memory_space=pltpu.SMEM), vmem, hbm, vmem, vmem, vmem, vmem, hbm, vmem,
+        ],
         out_specs=hbm,
         scratch_shapes=[
+            pltpu.VMEM((16, 64, PACKED), BF16),
             pltpu.VMEM((4, 16, 64, PACKED), BF16),
             pltpu.VMEM((1024, PACKED), BF16),
             pltpu.VMEM((1024, PACKED), F32),
@@ -488,87 +599,20 @@
             pltpu.VMEM((2, 2, 128, 128), BF16),
             pltpu.VMEM((8, 8, 128), F32),
             pltpu.VMEM((4, 2, 2, 128, 128), BF16),
-            dma((16,)), dma((192,)), dma((192,)),
+            pltpu.VMEM((4096, HD), BF16),
+            pltpu.VMEM((4096, 2 * HD), F32),
+            pltpu.VMEM((4096, HD), F32),
+            pltpu.VMEM((4096, HD), BF16),
+            dma((21,)), dma((COPIES,)), dma((COPIES,)),
         ],
         compiler_params=pltpu.CompilerParams(
-            collective_id=0, has_side_effects=True, vmem_limit_bytes=48 * 2**20
+            collective_id=0, has_side_effects=True, vmem_limit_bytes=61 * 2**20
         ),
         cost_estimate=pl.CostEstimate(
             flops=60_000_000_000, bytes_accessed=8_000_000, transcendentals=4_200_000
         ),
         name="front",
-    )(packed, wo, gain, live, merger, kvw, lm_gain)
-
-
-ROWS = 1024
-TILE = 256
-
-
-def lm_kernel(q, vis, span, bias, out):
-    step = pl.program_id(0)
-    scale = HD**-0.5 * LOG2E
-    keys = vis[:, :, 0].reshape(1024, HD)
-    ones = jnp.ones((1024, HD), BF16)
-    far_values = jnp.concatenate([vis[:, :, 1].reshape(1024, HD), ones], axis=1)
-    near_values = jnp.concatenate([span[1], ones[:512]], axis=1)
-    place = lax.broadcasted_iota(jnp.int32, (TILE, 512), 1)
-
-    def score(i):
-        query = q[pl.ds(i * TILE, TILE), :]
-        far = nt_dot(query, keys) + bias[...]
-        near = nt_dot(query, span[0])
-        row = lax.broadcasted_iota(jnp.int32, (TILE, 512), 0)
-        near = jnp.where(place <= (step * ROWS + i * TILE + row) // 8, near, MASKED)
-        top = jnp.maximum(
-            jnp.max(far, axis=1, keepdims=True), jnp.max(near, axis=1, keepdims=True)
-        )
-        return far, near, top
-
-    def blend(i, far, near, top):
-        far = jnp.exp2((far - top) * scale).astype(BF16)
-        near = jnp.exp2((near - top) * scale).astype(BF16)
-        total = jnp.dot(far, far_values, preferred_element_type=F32)
-        total += jnp.dot(near, near_values, preferred_element_type=F32)
-        out[pl.ds(i * TILE, TILE), :] = (total[:, :HD] / total[:, HD : HD + 1]).astype(BF16)
-
-    ready = score(0)
-    for i in range(ROWS // TILE):
-        following = score(i + 1) if i + 1 < ROWS // TILE else None
-        blend(i, *ready)
-        ready = following
-
-
-def lm_attention(q, vis, span, bias):
-    whole = lambda *shape: pl.BlockSpec(shape, lambda i: (0,) * len(shape))
-    rows = q.shape[0]
-    return pl.pallas_call(
-        lm_kernel,
-        out_shape=jax.ShapeDtypeStruct((rows, HD), BF16),
-        grid=(rows // ROWS,),
-        in_specs=[
-            pl.BlockSpec((ROWS, HD), lambda i: (i, 0)),
-            whole(4, 2, 2, 128, 128),
-            whole(2, 512, HD),
-            whole(1, 1024),
-        ],
-        out_specs=pl.BlockSpec((ROWS, HD), lambda i: (i, 0)),
-        compiler_params=pltpu.CompilerParams(vmem_limit_bytes=40 * 2**20),
-        name="lm",
-    )(q, vis, span, bias)
-
-
-def pack_patches(vit_qkv, patch_total, first_patch):
-    rows = vit_qkv.shape[1]
-    split = vit_qkv[0].reshape(rows, 3, VIT_HEADS, VIT_HDIM).transpose(1, 2, 0, 3)
-    ids = first_patch + jnp.arange(rows, dtype=jnp.int32)
-    live = ids < patch_total
-    mask = jnp.broadcast_to(
-        jnp.where(live, 0.0, MASKED).astype(BF16)[None, :, None], (VIT_HEADS, rows, 1)
-    )
-    one = jnp.ones((VIT_HEADS, rows, 1), BF16)
-    rest = jnp.zeros((VIT_HEADS, rows, PACKED - QUERY_AT - VIT_HDIM), BF16)
-    packed = jnp.concatenate([split[2], one, mask, split[1], split[0], rest], axis=-1)
-    return packed, live.astype(F32)[:, None]
+    )(counts, qkv, wo, gain, merger, kvw, lm_gain, queries, span)
 
 
 def local(
@@ -582,21 +626,12 @@
     queries,
     span_kv,
 ):
-    patch_total = patch_counts[0]
-    seq = lax.axis_index(SEQ)
-    tp = lax.axis_index(TP)
-    packed, live = pack_patches(vit_qkv, patch_total, (seq * 8 + tp) * vit_qkv.shape[1])
-    vis = visual_keys_values(
-        packed, vit_out_weight, vit_norm_gain[None], live,
-        merger_weight, kv_weight.T, lm_norm_gain[None],
-    )
-    key = jnp.arange(1024, dtype=jnp.int32)
-    block, r = key // 128, key % 128
-    token = (((block % 2) * 4 + r // 16 % 4) * 8 + (block // 2) * 2 + r // 64) * 16 + r % 16
-    bias = jnp.where(token < patch_total // 4, 0.0, MASKED)[None].astype(F32)
     rows = queries.shape[1] * queries.shape[2]
     span = span_kv[0, :, :, 0].transpose(1, 0, 2)
-    out = lm_attention(queries.reshape(rows, HD), vis, span, bias)
+    out = attend(
+        patch_counts, vit_qkv[0].transpose(1, 0, 2), vit_out_weight, vit_norm_gain[None],
+        merger_weight, kv_weight.T, lm_norm_gain[None], queries.reshape(rows, HD), span,
+    )
     return out.reshape(queries.shape)
 
 

time: 127 us -> 121 us (0.953)
  the two profiles are of different devices: /device:TPU:8 before, /device:TPU:6 now
where the time goes in v4:
time: 121 us
  Pallas kernels  115 us (95%)
  local copies, waits for them, and re-layouts  5.24 us (4%)
    pallas_call x1, Pallas kernels, attend(): pl.pallas_call(front_kernel, out_shape=jax.ShapeDtypeStruct(queries.shape...  115 us
    unnamed x2, local copies, waits for them, and re-layouts  3.95 us

profile of v4, /device:TPU:6, one launch (start us, length us, event | category | flops | bytes accessed | tf_op | source)
XLA Modules:
  0.0 120.7 jit_solution(10911857503694511618)
XLA Ops:
  0.7 1.3 %broadcast_in_dim.6.gain = f32[1,1280]{1,0:T(1,128)} reshape(f32[1280]{0:T(1024)} %param.12) | data formatting | bytes 10240 | tf_op jit(solution)/shard_map/broadcast_in_dim | solution.py:632
  1.9 1.7 %copy.12 = bf16[1,512,2,1,128]{4,1,2,3,0:T(8,128)(2,1)} copy(bf16[1,512,2,1,128]{4,2,3,1,0:T(2,128)(2,1)} %param.17) | data formatting | bytes 524288 | tf_op args[8]
  3.6 114.8 %front.1 = bf16[4096,128]{1,0:T(8,128)(2,1)} custom-call(s32[1]{0:T(128)S(6)} %copy.14.counts, bf16[3,64,1280]{2,1,0:T(8,128)(2,1)} %bitcast.15, bf16[1280,1280]{1,0:T(8,128)(2,1)} %wo.1, f32[1,1280]{1,0:T(1,128)} %broadcast_in_dim.6.gain, bf16[160,1024]{1,0:T(8,128)(2,1)} %merger.1, bf16[64,1024]{1,0:T(8,128)(2,1)} %bitcast.16, f32[1,1024]{1,0:T(1,128)} %bitcast.17, ...), custom_call_target="tpu_custom_call" | custom-call | flops 60000002048 | bytes 8000000 | tf_op jit(solution)/shard_map/front/pallas_call | solution.py:568
  118.4 2.3 %copy.15 = bf16[1,512,8,128]{3,2,1,0:T(8,128)(2,1)} copy(bf16[1,512,8,128]{3,2,1,0:T(8,128)(2,1)} %bitcast.12) | data formatting | bytes 2097152

commit v5 on v4

--- a/solution.py
+++ b/solution.py
@@ -22,7 +22,7 @@
 BF16 = jnp.bfloat16
 
 LOW = 16
-COPIES = 124
+COPIES = 130
 ONE_AT, MASK_AT, KEY_AT, QUERY_AT, PACKED = 80, 81, 82, 162, 256
 RING_ORDER = (0, 1, 7, 2, 6, 3, 5, 4)
 
@@ -193,7 +193,7 @@
             between(i)
             ready = following
 
-    for dz in (4, 3, 5, 2, 6, 1, 7, 0):
+    for dz in RING_ORDER:
         for dc in range(2):
             if (dz, dc) != (0, 0):
                 oz, oc_ = place(dz, dc)
@@ -289,9 +289,6 @@
         arrived(("y1", way, i), blocks_of(origin, dz))
 
     whole(down, False)
-    arrived(("w", "z"), mw.at[x, ozl])
-    go(("w", "e", 1), mw.at[x, ozl], mw.at[x, ozl], x=east)
-    go(("w", "w", 1), mw.at[x, ozl], mw.at[x, ozl], x=west)
     arrived(("k0", "e", 0), kw0.at[y, west, zl])
     go(("k0", "e", 2), kw0.at[y, west, zl], kw0.at[y, west, zl], x=east)
     arrived(("w", "e", 0), mw.at[west, zl])
@@ -315,16 +312,20 @@
                     zh=tile, zl=tzl, c=tc,
                 )
 
-    whole(across, False, [mod(zh + 1 + t, 4) for t in range(4)], give_back)
+    turns = (2, 1, 3, 0)
+    whole(across, False, [mod(zh + turn, 4) for turn in turns], give_back)
     att[me] = back[me]
 
+    arrived(("w", "z"), mw.at[x, ozl])
+    go(("w", "e", 1), mw.at[x, ozl], mw.at[x, ozl], x=east)
+    go(("w", "w", 1), mw.at[x, ozl], mw.at[x, ozl], x=west)
     for copy in weights:
         copy.wait()
     for t in range(4):
         for dzl in range(2):
             for dc in range(2):
                 if (t, dzl, dc) != (3, 0, 0):
-                    source = mod(zh + 3 - t, 4) * 4 + mod(zl + dzl, 2) * 2 + mod(c + dc, 2)
+                    source = mod(zh + 4 - turns[t], 4) * 4 + mod(zl + dzl, 2) * 2 + mod(c + dc, 2)
                     arrived(("o", t, dzl, dc), att.at[source])
 
     hidden = jnp.zeros((64, VIT_D), F32)
@@ -336,7 +337,7 @@
     hidden = jnp.where(live[:, :1], hidden, 0.0)
     centred = hidden - jnp.mean(hidden, axis=1, keepdims=True)
     spread = jnp.mean(centred * centred, axis=1, keepdims=True)
-    normed = (centred * lax.rsqrt(spread + 1e-6) * gain[...]).astype(BF16).astype(F32)
+    normed = (centred * lax.rsqrt(spread + 1e-6) * gain[...][None, :]).astype(BF16).astype(F32)
     for i in range(VIT_D // HD):
         nf[pl.ds(i * 64, 64), :] = normed[:, i * HD : (i + 1) * HD]
 
@@ -380,9 +381,12 @@
         arrived(("m", dy), mid.at[mod(y + 4 - dy, 4)])
 
     mine = zh * 2 + c
-    go("t0", mid, tok.at[mine], zh=right)
-    go("t1", mid, tok.at[mine], zh=left)
+    head, tail = pl.ds(0, 2), pl.ds(2, 2)
+    go("t0", mid.at[head], tok.at[mine, head], zh=right)
+    go("t1", mid.at[tail], tok.at[mine, tail], zh=left)
     go("t2", mid, tok.at[mine], c=oc)
+    go("t9", mid.at[tail], tok.at[mine, tail], zh=right)
+    go("t10", mid.at[head], tok.at[mine, head], zh=left)
     tok[mine] = mid[...]
     load_q.wait()
     near_part()
@@ -399,14 +403,15 @@
         go(("k1", way, k, 2), block, block, x=target)
 
     piece_on(0, y)
-    here = tok.at[left * 2 + c]
-    arrived("t0", here)
-    go("t3", here.at[pl.ds(0, 2)], here.at[pl.ds(0, 2)], zh=right)
+    here, there = tok.at[left * 2 + c], tok.at[right * 2 + c]
+    arrived("t0", here.at[head])
+    go("t3", here.at[head], here.at[head], zh=right)
+    arrived("t1", there.at[tail])
+    go("t5", there.at[tail], there.at[tail], zh=left)
+    arrived("t9", here.at[tail])
     go("t4", here, here, c=oc)
-    here = tok.at[right * 2 + c]
-    arrived("t1", here)
-    go("t5", here.at[pl.ds(2, 2)], here.at[pl.ds(2, 2)], zh=left)
-    go("t6", here, here, c=oc)
+    arrived("t10", there.at[head])
+    go("t6", there, there, c=oc)
     first, second = (tok.at[far * 2 + c].at[pl.ds(i, 2)] for i in (0, 2))
     arrived("t3", first)
     go("t7", first, first, c=oc)
@@ -436,18 +441,22 @@
     go("s0", sb.at[0, pl.ds(0, 64)], ra.at[0], y=up)
     go("s1", sb.at[0, pl.ds(64, 64)], ra.at[1], y=down)
     nxt, prv = part(up), part(down)
+    sb[1, 64:128] = nxt[64:128].astype(BF16)
+    sb[2, 0:64] = prv[0:64].astype(BF16)
+    go("s2", sb.at[1, pl.ds(64, 64)], rb.at[0, pl.ds(64, 64)], y=up)
+    go("s3", sb.at[2, pl.ds(0, 64)], rb.at[1, pl.ds(0, 64)], y=down)
     arrived("s0", ra.at[0])
     sb[1, 0:64] = (nxt[0:64] + ra[0].astype(F32)).astype(BF16)
-    sb[1, 64:128] = nxt[64:128].astype(BF16)
-    go("s2", sb.at[1], rb.at[0], y=up)
+    go("s4", sb.at[1, pl.ds(0, 64)], rb.at[0, pl.ds(0, 64)], y=up)
     arrived("s1", ra.at[1])
-    sb[2, 0:64] = prv[0:64].astype(BF16)
     sb[2, 64:128] = (prv[64:128] + ra[1].astype(F32)).astype(BF16)
-    go("s3", sb.at[2], rb.at[1], y=down)
+    go("s5", sb.at[2, pl.ds(64, 64)], rb.at[1, pl.ds(64, 64)], y=down)
     own = part(y)
     piece_on(3, across)
-    arrived("s2", rb.at[0])
-    arrived("s3", rb.at[1])
+    arrived("s2", rb.at[0, pl.ds(64, 64)])
+    arrived("s3", rb.at[1, pl.ds(0, 64)])
+    arrived("s4", rb.at[0, pl.ds(0, 64)])
+    arrived("s5", rb.at[1, pl.ds(64, 64)])
     embedded = (own + rb[0].astype(F32) + rb[1].astype(F32)).astype(BF16).astype(F32)
     square = jnp.sum(embedded * embedded, axis=1, keepdims=True)
     turned = jnp.transpose(jnp.broadcast_to(square, (128, 128)))
@@ -456,7 +465,7 @@
     for dzh, dc in others:
         slot = ssr.at[zh * 2 + c]
         go(("q", dzh, dc), slot, slot, zh=mod(zh + dzh, 4), c=mod(c + dc, 2))
-    scaled = (embedded * lm_gain[...]).astype(BF16)
+    scaled = (embedded * lm_gain[...][None, :]).astype(BF16)
     arrived(("k0", "u", 2), kw0.at[across, pl.ds(0, 2)])
     arrived(("k0", "d", 2), kw0.at[across, pl.ds(2, 2)])
     for k, row in enumerate((y, down, up, across)):
@@ -495,21 +504,25 @@
         ks[0, k] = term(far, k).astype(BF16)
     go("z0", ks.at[0, 0], ka.at[0], zh=right)
     go("z1", ks.at[0, 1], ka.at[1], zh=left)
+    ks[1, 1] = term(right, 1).astype(BF16)
+    ks[2, 0] = term(left, 0).astype(BF16)
+    go("z2", ks.at[1, 1], kb.at[0, 1], zh=right)
+    go("z3", ks.at[2, 0], kb.at[1, 0], zh=left)
     arrived("z0", ka.at[0])
     ks[1, 0] = (term(right, 0) + ka[0].astype(F32)).astype(BF16)
-    ks[1, 1] = term(right, 1).astype(BF16)
-    go("z2", ks.at[1], kb.at[0], zh=right)
+    go("z4", ks.at[1, 0], kb.at[0, 0], zh=right)
     arrived("z1", ka.at[1])
-    ks[2, 0] = term(left, 0).astype(BF16)
     ks[2, 1] = (term(left, 1) + ka[1].astype(F32)).astype(BF16)
-    go("z3", ks.at[2], kb.at[1], zh=left)
+    go("z5", ks.at[2, 1], kb.at[1, 1], zh=left)
     for dzh, dc in others:
         arrived(("q", dzh, dc), ssr.at[mod(zh + 4 - dzh, 4) * 2 + mod(c + dc, 2)])
     total = jnp.sum(ssr[...], axis=0)[0:1]
     factor = lax.rsqrt(jnp.broadcast_to(total, (128, 128)) / D + 1e-6)
     factor = jnp.transpose(factor)
-    arrived("z2", kb.at[0])
-    arrived("z3", kb.at[1])
+    arrived("z2", kb.at[0, 1])
+    arrived("z3", kb.at[1, 0])
+    arrived("z4", kb.at[0, 0])
+    arrived("z5", kb.at[1, 1])
     for k in range(2):
         done = term(zh, k) + kb[0, k].astype(F32) + kb[1, k].astype(F32)
         vis[y, zl, k] = (done * factor).astype(BF16)
@@ -629,8 +642,8 @@
     rows = queries.shape[1] * queries.shape[2]
     span = span_kv[0, :, :, 0].transpose(1, 0, 2)
     out = attend(
-        patch_counts, vit_qkv[0].transpose(1, 0, 2), vit_out_weight, vit_norm_gain[None],
-        merger_weight, kv_weight.T, lm_norm_gain[None], queries.reshape(rows, HD), span,
+        patch_counts, vit_qkv[0].transpose(1, 0, 2), vit_out_weight, vit_norm_gain,
+        merger_weight, kv_weight.T, lm_norm_gain, queries.reshape(rows, HD), span,
     )
     return out.reshape(queries.shape)
 

time: 121 us -> 109 us (0.901)
  the two profiles are of different devices: /device:TPU:6 before, /device:TPU:8 now
where the time goes in v5:
time: 109 us; the launch traced here: 108 us
  Pallas kernels  104 us (95%)
  local copies, waits for them, and re-layouts  3.95 us (4%)
    pallas_call x1, Pallas kernels, attend(): pl.pallas_call(front_kernel, out_shape=jax.ShapeDtypeStruct(queries.shape...  104 us
    unnamed x2, local copies, waits for them, and re-layouts  3.95 us

profile of v5, /device:TPU:8, one launch (start us, length us, event | category | flops | bytes accessed | tf_op | source)
XLA Modules:
  0.0 108.3 jit_solution(12773573745634003474)
XLA Ops:
  0.7 1.7 %copy.12 = bf16[1,512,2,1,128]{4,1,2,3,0:T(8,128)(2,1)} copy(bf16[1,512,2,1,128]{4,2,3,1,0:T(2,128)(2,1)} %param.17) | data formatting | bytes 524288 | tf_op args[8]
  2.3 103.7 %front.1 = bf16[4096,128]{1,0:T(8,128)(2,1)} custom-call(s32[1]{0:T(128)S(6)} %copy.14.counts, bf16[3,64,1280]{2,1,0:T(8,128)(2,1)} %bitcast.14, bf16[1280,1280]{1,0:T(8,128)(2,1)} %wo.1, f32[1280]{0:T(1024)} %gain.1, bf16[160,1024]{1,0:T(8,128)(2,1)} %merger.1, bf16[64,1024]{1,0:T(8,128)(2,1)} %bitcast.15, f32[1024]{0:T(1024)} %lm_gain.1, ...), custom_call_target="tpu_custom_call" | custom-call | flops 60000002048 | bytes 8000000 | tf_op jit(solution)/shard_map/front/pallas_call | solution.py:581
  106.1 2.3 %copy.15 = bf16[1,512,8,128]{3,2,1,0:T(8,128)(2,1)} copy(bf16[1,512,8,128]{3,2,1,0:T(8,128)(2,1)} %bitcast.11) | data formatting | bytes 2097152

commit v6 on v5

--- a/solution.py
+++ b/solution.py
@@ -319,6 +319,18 @@
     arrived(("w", "z"), mw.at[x, ozl])
     go(("w", "e", 1), mw.at[x, ozl], mw.at[x, ozl], x=east)
     go(("w", "w", 1), mw.at[x, ozl], mw.at[x, ozl], x=west)
+    arrived(("k1", "u"), kw1.at[x, down])
+    go(("k1", "u", 2), kw1.at[x, down, 0], kw1.at[x, down, 0], y=up)
+    piece(down, 1)
+    arrived(("k1", "d"), kw1.at[x, up])
+    go(("k1", "d", 2), kw1.at[x, up, 1], kw1.at[x, up, 1], y=down)
+    piece(up, 2)
+    arrived(("k0", "w", 0), kw0.at[y, east, zl])
+    arrived(("k0", "e", 1), kw0.at[y, west, ozl])
+    arrived(("k0", "e", 2), kw0.at[y, xfar, zl])
+    arrived(("k0", "w", 2), kw0.at[y, xfar, ozl])
+    go(("k0", "u"), kw0.at[y], kw0.at[y], y=up)
+    go(("k0", "d"), kw0.at[y], kw0.at[y], y=down)
     for copy in weights:
         copy.wait()
     for t in range(4):
@@ -365,18 +377,6 @@
 
     arrived(("w", "w", 1), mw.at[east, ozl])
     go(("w", "w", 2), mw.at[east, ozl], mw.at[east, ozl], x=west)
-    arrived(("k1", "u"), kw1.at[x, down])
-    go(("k1", "u", 2), kw1.at[x, down, 0], kw1.at[x, down, 0], y=up)
-    piece(down, 1)
-    arrived(("k1", "d"), kw1.at[x, up])
-    go(("k1", "d", 2), kw1.at[x, up, 1], kw1.at[x, up, 1], y=down)
-    piece(up, 2)
-    arrived(("k0", "w", 0), kw0.at[y, east, zl])
-    arrived(("k0", "e", 1), kw0.at[y, west, ozl])
-    arrived(("k0", "e", 2), kw0.at[y, xfar, zl])
-    arrived(("k0", "w", 2), kw0.at[y, xfar, ozl])
-    go(("k0", "u"), kw0.at[y], kw0.at[y], y=up)
-    go(("k0", "d"), kw0.at[y], kw0.at[y], y=down)
     for dy in range(1, 4):
         arrived(("m", dy), mid.at[mod(y + 4 - dy, 4)])
 
@@ -402,7 +402,13 @@
         arrived(("k1", way, k), block)
         go(("k1", way, k, 2), block, block, x=target)
 
+    arrived(("k0", "u"), kw0.at[down])
+    go(("k0", "u", 2), kw0.at[down, pl.ds(0, 2)], kw0.at[down, pl.ds(0, 2)], y=up)
+    arrived(("k0", "d"), kw0.at[up])
+    go(("k0", "d", 2), kw0.at[up, pl.ds(2, 2)], kw0.at[up, pl.ds(2, 2)], y=down)
     piece_on(0, y)
+    piece_on(1, down)
+    piece_on(2, up)
     here, there = tok.at[left * 2 + c], tok.at[right * 2 + c]
     arrived("t0", here.at[head])
     go("t3", here.at[head], here.at[head], zh=right)
@@ -417,12 +423,6 @@
     go("t7", first, first, c=oc)
     arrived("t5", second)
     go("t8", second, second, c=oc)
-    piece_on(1, down)
-    piece_on(2, up)
-    arrived(("k0", "u"), kw0.at[down])
-    go(("k0", "u", 2), kw0.at[down, pl.ds(0, 2)], kw0.at[down, pl.ds(0, 2)], y=up)
-    arrived(("k0", "d"), kw0.at[up])
-    go(("k0", "d", 2), kw0.at[up, pl.ds(2, 2)], kw0.at[up, pl.ds(2, 2)], y=down)
     arrived("t2", tok.at[zh * 2 + oc])
     arrived("t4", tok.at[left * 2 + oc])
     arrived("t6", tok.at[right * 2 + oc])
@@ -445,6 +445,7 @@
     sb[2, 0:64] = prv[0:64].astype(BF16)
     go("s2", sb.at[1, pl.ds(64, 64)], rb.at[0, pl.ds(64, 64)], y=up)
     go("s3", sb.at[2, pl.ds(0, 64)], rb.at[1, pl.ds(0, 64)], y=down)
+    piece_on(3, across)
     arrived("s0", ra.at[0])
     sb[1, 0:64] = (nxt[0:64] + ra[0].astype(F32)).astype(BF16)
     go("s4", sb.at[1, pl.ds(0, 64)], rb.at[0, pl.ds(0, 64)], y=up)
@@ -452,7 +453,6 @@
     sb[2, 64:128] = (prv[64:128] + ra[1].astype(F32)).astype(BF16)
     go("s5", sb.at[2, pl.ds(64, 64)], rb.at[1, pl.ds(64, 64)], y=down)
     own = part(y)
-    piece_on(3, across)
     arrived("s2", rb.at[0, pl.ds(64, 64)])
     arrived("s3", rb.at[1, pl.ds(0, 64)])
     arrived("s4", rb.at[0, pl.ds(0, 64)])

time: 109 us -> 109 us (level)
  no operation moved by 1% of the time
where the time goes in v6:
time: 109 us; the launch traced here: 108 us
  Pallas kernels  104 us (95%)
  local copies, waits for them, and re-layouts  3.95 us (4%)
    pallas_call x1, Pallas kernels, attend(): pl.pallas_call(front_kernel, out_shape=jax.ShapeDtypeStruct(queries.shape...  104 us
    unnamed x2, local copies, waits for them, and re-layouts  3.95 us

profile of v6, /device:TPU:8, one launch (start us, length us, event | category | flops | bytes accessed | tf_op | source)
XLA Modules:
  0.0 108.4 jit_solution(7778789470151516365)
XLA Ops:
  0.7 1.7 %copy.12 = bf16[1,512,2,1,128]{4,1,2,3,0:T(8,128)(2,1)} copy(bf16[1,512,2,1,128]{4,2,3,1,0:T(2,128)(2,1)} %param.17) | data formatting | bytes 524288 | tf_op args[8]
  2.3 103.8 %front.1 = bf16[4096,128]{1,0:T(8,128)(2,1)} custom-call(s32[1]{0:T(128)S(6)} %copy.14.counts, bf16[3,64,1280]{2,1,0:T(8,128)(2,1)} %bitcast.14, bf16[1280,1280]{1,0:T(8,128)(2,1)} %wo.1, f32[1280]{0:T(1024)} %gain.1, bf16[160,1024]{1,0:T(8,128)(2,1)} %merger.1, bf16[64,1024]{1,0:T(8,128)(2,1)} %bitcast.15, f32[1024]{0:T(1024)} %lm_gain.1, ...), custom_call_target="tpu_custom_call" | custom-call | flops 60000002048 | bytes 8000000 | tf_op jit(solution)/shard_map/front/pallas_call | solution.py:581
  106.1 2.3 %copy.15 = bf16[1,512,8,128]{3,2,1,0:T(8,128)(2,1)} copy(bf16[1,512,8,128]{3,2,1,0:T(8,128)(2,1)} %bitcast.11) | data formatting | bytes 2097152
